TPU v7x, 256 devices: a whole 4x4x8 slice. The times are simulated.
256 devices in a mesh: slab: 128 (over x, z, y), sub: 2 (over core).
Axes of the slice: x: 4, y: 4, z: 8, core: 2. Of those that a mesh axis runs over, the one named last changes fastest.
Arguments:
- position: float32 [3, 65536, 128], P(None, ('slab', 'sub')), may hold values from -6 to 6
- state: int32 [65536, 128], P(('slab', 'sub')), may hold values from 0 to 2, as said below
- neighbours: int32 [65536, 8], P(('slab', 'sub')), may hold values from 0 to 65535, as said below
- voxel: int32 [65536, 128], P(('slab', 'sub')), may hold values from 0 to 33554431, as said below
- substrate: float32 [1024, 128, 256], P('slab', 'sub'), may hold values from 0.5 to 1.5
- secretion: float32 [1024, 128, 256], P('slab', 'sub'), may hold values from 0.2 to 4
Outputs:
- new_position: float32 [3, 65536, 128], P(None, ('slab', 'sub'))
- new_substrate: float32 [1024, 128, 256], P('slab', 'sub')
- necrotic_fraction: float32 [], replicated
Inputs may be any that keep to these rules, and one draw needn't show every extreme that they name: `state`: 0 marks an empty slot, 1 a live cell, 2 a necrotic cell. `neighbours`: with tiles in blocks of 256 (block t // 256, its slab the block // 2, its part the block % 2): tile t lists itself first, then 8 - 1 different other tiles, each of its own block, of the last 32 tiles of the block 2 blocks before, or of the first 32 tiles of the block 2 blocks after. `voxel`: the cells of a tile of slab s and part u lie in voxels with x from s * 8 to s * 8 + 7 and y from u * 64 to u * 64 + 63.
All inputs are finite; a program needn't handle non-finite values.
Results may differ from a plain program's by a relative error of at most 0.00002.
Values sent between devices are 32-bit elements; how exact they have to be, the bound alone decides.
No kernel may reach another device: no remote copies, remote signals or barrier semaphores. Data moves between devices by JAX's collectives and lax.ppermute only.
A program may use at most 64 MiB of HBM per device.

v0:
```python
import jax
import jax.numpy as jnp
from jax import lax
from jax.sharding import Mesh
from jax.sharding import PartitionSpec as P

TILE = 128
NB = 8
GHOST = 32
SWEEPS = 8
SLAB = ("slab_0", "slab_1", "slab_2")
SLAB_SUB = ("slab_0", "slab_1", "slab_2", "sub")


SOFTENING = 0.01
REPEL_RADIUS = 2.0
ADHERE_RADIUS = 3.0
REPEL_STRENGTH = 0.05
ADHERE_STRENGTH = 0.02
SPEED_LIMIT = 0.2
SPEED_EPSILON = 1e-06
SUBSTRATE_STEP = 0.5
DECAY_RATE = 0.1
DIFFUSION_NUMBER = 2.0
UPTAKE_SCALE = 0.25


def with_halo(x, sides, width):
    for axis, dim in sides:
        size, length = (lax.axis_size(axis), x.shape[dim])
        up = [(i, (i + 1) % size) for i in range(size - 1)]
        down = [(j, i) for i, j in up]
        last = lax.slice_in_dim(x, length - width, length, axis=dim)
        initial = lax.slice_in_dim(x, 0, width, axis=dim)
        before = lax.ppermute(last, axis, up)
        after = lax.ppermute(initial, axis, down)
        x = jnp.concatenate([before, x, after], axis=dim)
    return x


def combined_by_axis(x, axes, combine):
    for axis in axes:
        pieces = jax.tree.map(lambda part: lax.all_gather(part, axis), x)
        x = jax.tree.map(lambda part: part[0], pieces)
        for k in range(1, lax.axis_size(axis)):
            x = combine(x, jax.tree.map(lambda part: part[k], pieces))
    return x


def pair_forces(own_tiles, others):
    delta_x = own_tiles[0][:, :, None] - others[0][:, None, :]
    delta_y = own_tiles[1][:, :, None] - others[1][:, None, :]
    delta_z = own_tiles[2][:, :, None] - others[2][:, None, :]
    distance = jnp.sqrt(delta_x * delta_x + delta_y * delta_y + delta_z * delta_z + SOFTENING)
    repel = REPEL_STRENGTH * jnp.square(jnp.maximum(0.0, 1.0 - distance / REPEL_RADIUS))
    adhere = (
        ADHERE_STRENGTH
        * jnp.square(jnp.maximum(0.0, 1.0 - distance / ADHERE_RADIUS))
        * (own_tiles[4][:, :, None] * others[4][:, None, :])
    )
    weight = own_tiles[3][:, :, None] * others[3][:, None, :] * (repel - adhere) / distance
    return jnp.stack(
        [
            jnp.sum(weight * delta_x, -1),
            jnp.sum(weight * delta_y, -1),
            jnp.sum(weight * delta_z, -1),
        ],
        0,
    )


def neighbour_sum(padded):
    center = padded[1:-1, 1:-1]
    along_z = jnp.pad(center, ((0, 0), (0, 0), (1, 1)))
    return (
        padded[2:, 1:-1]
        + padded[:-2, 1:-1]
        + padded[1:-1, 2:]
        + padded[1:-1, :-2]
        + along_z[:, :, 2:]
        + along_z[:, :, :-2]
    )


def combine_stats(earlier, later):
    return (jnp.maximum(earlier[0], later[0]), earlier[1] + later[1], earlier[2] + later[2])


def body(position, state, neighbours, voxel, substrate, secretion):
    tiles_dev = position.shape[1]
    sub_count = lax.axis_size("sub")
    slab_count = lax.axis_size(SLAB)
    slab_index = lax.axis_index(SLAB)
    sub_index = lax.axis_index("sub")
    occupied = (state > 0).astype(jnp.float32)
    living = (state == 1).astype(jnp.float32)
    live_local = jnp.sum((state == 1).astype(jnp.int32))
    necrotic_local = jnp.sum((state == 2).astype(jnp.int32))
    features = jnp.concatenate([position, occupied[None], living[None]], 0)
    codes = jnp.concatenate([position, state.astype(jnp.float32)[None]], 0)
    ghost_codes = with_halo(codes, ((SLAB, 1),), GHOST)
    ghost_state = ghost_codes[3]
    ghosted = jnp.concatenate(
        [
            ghost_codes[:3],
            (ghost_state > 0.5).astype(jnp.float32)[None],
            (ghost_state == 1.0).astype(jnp.float32)[None],
        ],
        0,
    )
    first_tile = (slab_index * sub_count + sub_index) * tiles_dev
    below_block = neighbours < first_tile
    above_block = neighbours >= first_tile + tiles_dev
    local_ids = jnp.where(
        below_block,
        neighbours - (first_tile - sub_count * tiles_dev) - (tiles_dev - GHOST),
        jnp.where(
            above_block,
            GHOST + tiles_dev + neighbours - (first_tile + sub_count * tiles_dev),
            GHOST + neighbours - first_tile,
        ),
    )
    group_size = 4
    while tiles_dev % (2 * group_size) == 0 and tiles_dev // group_size > 16:
        group_size = 2 * group_size
    rounds = tiles_dev // group_size
    own_blocks = features.reshape(5, rounds, group_size, TILE).transpose(1, 0, 2, 3)
    id_blocks = local_ids.reshape(rounds, group_size, NB)

    def one_block(block_item):
        own_tiles, tile_ids = block_item
        others = jnp.take(ghosted, tile_ids.reshape(-1), axis=1).reshape(5, group_size, NB * TILE)
        return pair_forces(own_tiles, others)

    forces = lax.map(one_block, (own_blocks, id_blocks))
    velocity = forces.transpose(1, 0, 2, 3).reshape(3, tiles_dev, TILE)
    cell_speed = jnp.sqrt(jnp.sum(velocity * velocity, 0))
    local_fastest = jnp.max(cell_speed)
    fastest, live_float, necrotic_float = combined_by_axis(
        (local_fastest, live_local.astype(jnp.float32), necrotic_local.astype(jnp.float32)),
        SLAB_SUB,
        combine_stats,
    )
    size_x, size_y, size_z = substrate.shape
    grid_y = size_y * sub_count
    grid_total = size_x * slab_count * grid_y * size_z
    per_cell = UPTAKE_SCALE * grid_total / live_float
    voxel_x = voxel // (grid_y * size_z)
    voxel_y = voxel // size_z % grid_y
    voxel_z = voxel % size_z
    local_flat = (
        (voxel_x - slab_index * size_x) * size_y + (voxel_y - sub_index * size_y)
    ) * size_z + voxel_z
    cell_count = (
        jnp.zeros((size_x * size_y * size_z,), jnp.float32)
        .at[local_flat.reshape(-1)]
        .add(living.reshape(-1))
        .reshape(size_x, size_y, size_z)
    )
    diagonal = 1.0 + SUBSTRATE_STEP * DECAY_RATE + 6.0 * DIFFUSION_NUMBER + per_cell * cell_count
    right_side = substrate + SUBSTRATE_STEP * secretion
    concentration = substrate
    margin_terms = with_halo(jnp.stack([right_side, diagonal]), ((SLAB, 1), ("sub", 2)), 2)
    row_index = slab_index * size_x - 1 + jnp.arange(size_x + 2)
    column_index = sub_index * size_y - 1 + jnp.arange(size_y + 2)
    inside_x = (row_index >= 0) & (row_index < size_x * slab_count)
    inside_y = (column_index >= 0) & (column_index < grid_y)
    inside = inside_x[:, None, None] & inside_y[None, :, None]
    right_margin = margin_terms[0][1:-1, 1:-1]
    diagonal_margin = jnp.where(inside, margin_terms[1][1:-1, 1:-1], 1.0)
    for pair_index in range(SWEEPS // 2):
        padded = with_halo(concentration, ((SLAB, 0), ("sub", 1)), 2)
        middle = jnp.where(
            inside, (right_margin + DIFFUSION_NUMBER * neighbour_sum(padded)) / diagonal_margin, 0.0
        )
        concentration = (right_side + DIFFUSION_NUMBER * neighbour_sum(middle)) / diagonal
    step_size = SPEED_LIMIT / (fastest + SPEED_EPSILON)
    new_position = position + step_size * velocity
    necrotic_fraction = necrotic_float / (live_float + necrotic_float)
    return (new_position, concentration, necrotic_fraction)


def solution(mesh):
    finer = Mesh(
        mesh.devices.reshape(4, 8, 4, mesh.shape["sub"]), ("slab_0", "slab_1", "slab_2", "sub")
    )
    placed = (
        P(None, SLAB_SUB, None),
        P(SLAB_SUB, None),
        P(SLAB_SUB, None),
        P(SLAB_SUB, None),
        P(SLAB, "sub", None),
        P(SLAB, "sub", None),
    )
    return jax.shard_map(
        body,
        mesh=finer,
        in_specs=placed,
        out_specs=(P(None, SLAB_SUB, None), P(SLAB, "sub", None), P()),
        check_vma=False,
    )
```

profile of v0, /device:TPU:1, one launch (start us, length us, event | category | flops | bytes accessed | tf_op | source)
XLA Modules:
  0.0 598.8 jit_solution(3362955649233514030)
XLA Ops:
  0.7 1.7 fusion.77
  2.4 1.4 collective-permute-start.7
  3.8 5.3 collective-permute-start.6
  9.1 1.6 convert_reduce_fusion
  12.1 2.7 collective-permute-start
  14.8 1.3 collective-permute-start.1
  22.6 262.8 %while.10 = (s32[]{:T(128)}, f32[16,3,16,128]{3,2,1,0:T(8,128)S(1)}, f32[16,5,16,128]{3,2,0,1:T(8,128)S(1)}, s32[16,16,8]{2,1,0:T(8,128)S(1)}, f32[5,320,128]{2,0,1:T(8,128)S(1)}, /*index=5*/s32[]{:T(128)}) while((s32[]{:T(128)}, f32[16,3,16,128]{3,2,1,0:T(8,128)S(1)}, f32[16,5,16,128]{3,2,0,1:T(8,128)S(1)}, s32[16,16,8]{2,1,0:T(8,128)S(1)}, ...), condition=%wide.region_4.5_spmd, body=%wide.region_0.4_spmd.sunk | while | flops 65101952 | bytes 3237721 | solution.py:135
  24.8 14.1 %fusion.85 = (f32[16,128]{1,0:T(8,128)S(1)}, f32[16,128]{1,0:T(8,128)S(1)}, f32[16,128]{1,0:T(8,128)S(1)}) fusion(f32[16,1024]{1,0:T(8,128)S(1)} %sub.306, f32[16,128]{1,0:T(8,128)S(1)} %get-tuple-element.162, f32[16,1024]{1,0:T(8,128)S(1)} %mul.396, f32[16,128]{1,0:T(8,128)S(1)} %get-tuple-element.164, f32[16,1024]{1,0:T(8,128)S(1)} %sub.307, ...), kind=kLoop, calls=%fused_computation.12.clone.1 | loop fusion | flops 65005568 | bytes 393216 | tf_op jit(solution)/shard_map/while/body/eval_jaxpr/reduce_sum | solution.py:64
  41.3 14.1 %fusion.85 = (f32[16,128]{1,0:T(8,128)S(1)}, f32[16,128]{1,0:T(8,128)S(1)}, f32[16,128]{1,0:T(8,128)S(1)}) fusion(f32[16,1024]{1,0:T(8,128)S(1)} %sub.306, f32[16,128]{1,0:T(8,128)S(1)} %get-tuple-element.162, f32[16,1024]{1,0:T(8,128)S(1)} %mul.396, f32[16,128]{1,0:T(8,128)S(1)} %get-tuple-element.164, f32[16,1024]{1,0:T(8,128)S(1)} %sub.307, ...), kind=kLoop, calls=%fused_computation.12.clone.1 | loop fusion | flops 65005568 | bytes 393216 | tf_op jit(solution)/shard_map/while/body/eval_jaxpr/reduce_sum | solution.py:64
  57.7 14.1 %fusion.85 = (f32[16,128]{1,0:T(8,128)S(1)}, f32[16,128]{1,0:T(8,128)S(1)}, f32[16,128]{1,0:T(8,128)S(1)}) fusion(f32[16,1024]{1,0:T(8,128)S(1)} %sub.306, f32[16,128]{1,0:T(8,128)S(1)} %get-tuple-element.162, f32[16,1024]{1,0:T(8,128)S(1)} %mul.396, f32[16,128]{1,0:T(8,128)S(1)} %get-tuple-element.164, f32[16,1024]{1,0:T(8,128)S(1)} %sub.307, ...), kind=kLoop, calls=%fused_computation.12.clone.1 | loop fusion | flops 65005568 | bytes 393216 | tf_op jit(solution)/shard_map/while/body/eval_jaxpr/reduce_sum | solution.py:64
  74.1 14.1 %fusion.85 = (f32[16,128]{1,0:T(8,128)S(1)}, f32[16,128]{1,0:T(8,128)S(1)}, f32[16,128]{1,0:T(8,128)S(1)}) fusion(f32[16,1024]{1,0:T(8,128)S(1)} %sub.306, f32[16,128]{1,0:T(8,128)S(1)} %get-tuple-element.162, f32[16,1024]{1,0:T(8,128)S(1)} %mul.396, f32[16,128]{1,0:T(8,128)S(1)} %get-tuple-element.164, f32[16,1024]{1,0:T(8,128)S(1)} %sub.307, ...), kind=kLoop, calls=%fused_computation.12.clone.1 | loop fusion | flops 65005568 | bytes 393216 | tf_op jit(solution)/shard_map/while/body/eval_jaxpr/reduce_sum | solution.py:64
  90.5 14.1 %fusion.85 = (f32[16,128]{1,0:T(8,128)S(1)}, f32[16,128]{1,0:T(8,128)S(1)}, f32[16,128]{1,0:T(8,128)S(1)}) fusion(f32[16,1024]{1,0:T(8,128)S(1)} %sub.306, f32[16,128]{1,0:T(8,128)S(1)} %get-tuple-element.162, f32[16,1024]{1,0:T(8,128)S(1)} %mul.396, f32[16,128]{1,0:T(8,128)S(1)} %get-tuple-element.164, f32[16,1024]{1,0:T(8,128)S(1)} %sub.307, ...), kind=kLoop, calls=%fused_computation.12.clone.1 | loop fusion | flops 65005568 | bytes 393216 | tf_op jit(solution)/shard_map/while/body/eval_jaxpr/reduce_sum | solution.py:64
  107.0 14.1 %fusion.85 = (f32[16,128]{1,0:T(8,128)S(1)}, f32[16,128]{1,0:T(8,128)S(1)}, f32[16,128]{1,0:T(8,128)S(1)}) fusion(f32[16,1024]{1,0:T(8,128)S(1)} %sub.306, f32[16,128]{1,0:T(8,128)S(1)} %get-tuple-element.162, f32[16,1024]{1,0:T(8,128)S(1)} %mul.396, f32[16,128]{1,0:T(8,128)S(1)} %get-tuple-element.164, f32[16,1024]{1,0:T(8,128)S(1)} %sub.307, ...), kind=kLoop, calls=%fused_computation.12.clone.1 | loop fusion | flops 65005568 | bytes 393216 | tf_op jit(solution)/shard_map/while/body/eval_jaxpr/reduce_sum | solution.py:64
  123.4 14.1 %fusion.85 = (f32[16,128]{1,0:T(8,128)S(1)}, f32[16,128]{1,0:T(8,128)S(1)}, f32[16,128]{1,0:T(8,128)S(1)}) fusion(f32[16,1024]{1,0:T(8,128)S(1)} %sub.306, f32[16,128]{1,0:T(8,128)S(1)} %get-tuple-element.162, f32[16,1024]{1,0:T(8,128)S(1)} %mul.396, f32[16,128]{1,0:T(8,128)S(1)} %get-tuple-element.164, f32[16,1024]{1,0:T(8,128)S(1)} %sub.307, ...), kind=kLoop, calls=%fused_computation.12.clone.1 | loop fusion | flops 65005568 | bytes 393216 | tf_op jit(solution)/shard_map/while/body/eval_jaxpr/reduce_sum | solution.py:64
  139.8 14.1 %fusion.85 = (f32[16,128]{1,0:T(8,128)S(1)}, f32[16,128]{1,0:T(8,128)S(1)}, f32[16,128]{1,0:T(8,128)S(1)}) fusion(f32[16,1024]{1,0:T(8,128)S(1)} %sub.306, f32[16,128]{1,0:T(8,128)S(1)} %get-tuple-element.162, f32[16,1024]{1,0:T(8,128)S(1)} %mul.396, f32[16,128]{1,0:T(8,128)S(1)} %get-tuple-element.164, f32[16,1024]{1,0:T(8,128)S(1)} %sub.307, ...), kind=kLoop, calls=%fused_computation.12.clone.1 | loop fusion | flops 65005568 | bytes 393216 | tf_op jit(solution)/shard_map/while/body/eval_jaxpr/reduce_sum | solution.py:64
  156.2 14.1 %fusion.85 = (f32[16,128]{1,0:T(8,128)S(1)}, f32[16,128]{1,0:T(8,128)S(1)}, f32[16,128]{1,0:T(8,128)S(1)}) fusion(f32[16,1024]{1,0:T(8,128)S(1)} %sub.306, f32[16,128]{1,0:T(8,128)S(1)} %get-tuple-element.162, f32[16,1024]{1,0:T(8,128)S(1)} %mul.396, f32[16,128]{1,0:T(8,128)S(1)} %get-tuple-element.164, f32[16,1024]{1,0:T(8,128)S(1)} %sub.307, ...), kind=kLoop, calls=%fused_computation.12.clone.1 | loop fusion | flops 65005568 | bytes 393216 | tf_op jit(solution)/shard_map/while/body/eval_jaxpr/reduce_sum | solution.py:64
  172.7 14.1 %fusion.85 = (f32[16,128]{1,0:T(8,128)S(1)}, f32[16,128]{1,0:T(8,128)S(1)}, f32[16,128]{1,0:T(8,128)S(1)}) fusion(f32[16,1024]{1,0:T(8,128)S(1)} %sub.306, f32[16,128]{1,0:T(8,128)S(1)} %get-tuple-element.162, f32[16,1024]{1,0:T(8,128)S(1)} %mul.396, f32[16,128]{1,0:T(8,128)S(1)} %get-tuple-element.164, f32[16,1024]{1,0:T(8,128)S(1)} %sub.307, ...), kind=kLoop, calls=%fused_computation.12.clone.1 | loop fusion | flops 65005568 | bytes 393216 | tf_op jit(solution)/shard_map/while/body/eval_jaxpr/reduce_sum | solution.py:64
  189.1 14.1 %fusion.85 = (f32[16,128]{1,0:T(8,128)S(1)}, f32[16,128]{1,0:T(8,128)S(1)}, f32[16,128]{1,0:T(8,128)S(1)}) fusion(f32[16,1024]{1,0:T(8,128)S(1)} %sub.306, f32[16,128]{1,0:T(8,128)S(1)} %get-tuple-element.162, f32[16,1024]{1,0:T(8,128)S(1)} %mul.396, f32[16,128]{1,0:T(8,128)S(1)} %get-tuple-element.164, f32[16,1024]{1,0:T(8,128)S(1)} %sub.307, ...), kind=kLoop, calls=%fused_computation.12.clone.1 | loop fusion | flops 65005568 | bytes 393216 | tf_op jit(solution)/shard_map/while/body/eval_jaxpr/reduce_sum | solution.py:64
  205.5 14.1 %fusion.85 = (f32[16,128]{1,0:T(8,128)S(1)}, f32[16,128]{1,0:T(8,128)S(1)}, f32[16,128]{1,0:T(8,128)S(1)}) fusion(f32[16,1024]{1,0:T(8,128)S(1)} %sub.306, f32[16,128]{1,0:T(8,128)S(1)} %get-tuple-element.162, f32[16,1024]{1,0:T(8,128)S(1)} %mul.396, f32[16,128]{1,0:T(8,128)S(1)} %get-tuple-element.164, f32[16,1024]{1,0:T(8,128)S(1)} %sub.307, ...), kind=kLoop, calls=%fused_computation.12.clone.1 | loop fusion | flops 65005568 | bytes 393216 | tf_op jit(solution)/shard_map/while/body/eval_jaxpr/reduce_sum | solution.py:64
  221.9 14.1 %fusion.85 = (f32[16,128]{1,0:T(8,128)S(1)}, f32[16,128]{1,0:T(8,128)S(1)}, f32[16,128]{1,0:T(8,128)S(1)}) fusion(f32[16,1024]{1,0:T(8,128)S(1)} %sub.306, f32[16,128]{1,0:T(8,128)S(1)} %get-tuple-element.162, f32[16,1024]{1,0:T(8,128)S(1)} %mul.396, f32[16,128]{1,0:T(8,128)S(1)} %get-tuple-element.164, f32[16,1024]{1,0:T(8,128)S(1)} %sub.307, ...), kind=kLoop, calls=%fused_computation.12.clone.1 | loop fusion | flops 65005568 | bytes 393216 | tf_op jit(solution)/shard_map/while/body/eval_jaxpr/reduce_sum | solution.py:64
  238.4 14.1 %fusion.85 = (f32[16,128]{1,0:T(8,128)S(1)}, f32[16,128]{1,0:T(8,128)S(1)}, f32[16,128]{1,0:T(8,128)S(1)}) fusion(f32[16,1024]{1,0:T(8,128)S(1)} %sub.306, f32[16,128]{1,0:T(8,128)S(1)} %get-tuple-element.162, f32[16,1024]{1,0:T(8,128)S(1)} %mul.396, f32[16,128]{1,0:T(8,128)S(1)} %get-tuple-element.164, f32[16,1024]{1,0:T(8,128)S(1)} %sub.307, ...), kind=kLoop, calls=%fused_computation.12.clone.1 | loop fusion | flops 65005568 | bytes 393216 | tf_op jit(solution)/shard_map/while/body/eval_jaxpr/reduce_sum | solution.py:64
  254.8 14.1 %fusion.85 = (f32[16,128]{1,0:T(8,128)S(1)}, f32[16,128]{1,0:T(8,128)S(1)}, f32[16,128]{1,0:T(8,128)S(1)}) fusion(f32[16,1024]{1,0:T(8,128)S(1)} %sub.306, f32[16,128]{1,0:T(8,128)S(1)} %get-tuple-element.162, f32[16,1024]{1,0:T(8,128)S(1)} %mul.396, f32[16,128]{1,0:T(8,128)S(1)} %get-tuple-element.164, f32[16,1024]{1,0:T(8,128)S(1)} %sub.307, ...), kind=kLoop, calls=%fused_computation.12.clone.1 | loop fusion | flops 65005568 | bytes 393216 | tf_op jit(solution)/shard_map/while/body/eval_jaxpr/reduce_sum | solution.py:64
  271.2 14.1 %fusion.85 = (f32[16,128]{1,0:T(8,128)S(1)}, f32[16,128]{1,0:T(8,128)S(1)}, f32[16,128]{1,0:T(8,128)S(1)}) fusion(f32[16,1024]{1,0:T(8,128)S(1)} %sub.306, f32[16,128]{1,0:T(8,128)S(1)} %get-tuple-element.162, f32[16,1024]{1,0:T(8,128)S(1)} %mul.396, f32[16,128]{1,0:T(8,128)S(1)} %get-tuple-element.164, f32[16,1024]{1,0:T(8,128)S(1)} %sub.307, ...), kind=kLoop, calls=%fused_computation.12.clone.1 | loop fusion | flops 65005568 | bytes 393216 | tf_op jit(solution)/shard_map/while/body/eval_jaxpr/reduce_sum | solution.py:64
  286.1 1.4 dynamic-update-slice
  288.1 20.3 %all-reduce.22 = (f32[4]{0:T(128)S(1)}, f32[4]{0:T(128)S(1)}, f32[4]{0:T(128)S(1)}) all-reduce(f32[4]{0:T(128)S(1)} %dynamic-update-slice, f32[4]{0:T(128)S(1)} %dynamic-update-slice.4, f32[4]{0:T(128)S(1)} %dynamic-update-slice.8), channel_id=1, replica_groups=mesh['slab_0'=4,'slab_1'=8,'slab_2'=4,'sub'=2] {'slab_0'}, use_global_device_ids=true, to_apply=%add.8 | all-reduce | flops 12 | bytes 96
  311.4 10.9 %all-reduce.20 = (f32[8]{0:T(128)S(1)}, f32[8]{0:T(128)S(1)}, f32[8]{0:T(128)S(1)}) all-reduce(f32[8]{0:T(128)S(1)} %maximum_dynamic-update-slice_fusion.2, f32[8]{0:T(128)S(1)} %add_dynamic-update-slice_fusion.5, f32[8]{0:T(128)S(1)} %add_dynamic-update-slice_fusion.3), channel_id=1, replica_groups=mesh['slab_0'=4,'slab_1'=8,'slab_2'=4,'sub'=2] {'slab_1'}, use_global_device_ids=true, to_apply=%add.9 | all-reduce | flops 24 | bytes 192
  325.4 6.7 %all-reduce.21 = (f32[4]{0:T(128)S(1)}, f32[4]{0:T(128)S(1)}, f32[4]{0:T(128)S(1)}) all-reduce(f32[4]{0:T(128)S(1)} %maximum_dynamic-update-slice_fusion, f32[4]{0:T(128)S(1)} %add_dynamic-update-slice_fusion.1, f32[4]{0:T(128)S(1)} %add_dynamic-update-slice_fusion), channel_id=1, replica_groups=mesh['slab_0'=4,'slab_1'=8,'slab_2'=4,'sub'=2] {'slab_2'}, use_global_device_ids=true, to_apply=%add.10 | all-reduce | flops 12 | bytes 96
  334.5 171.2 %scatter_custom_fusion = f32[131072]{0:T(1024)S(1)} fusion(s32[32768]{0:T(1024)S(1)} %bitcast.85, f32[32768]{0:T(1024)S(1)} %get-tuple-element.71, f32[]{:T(128)} %constant.140.clone.1), kind=kCustom, calls=%fused_computation.161 | custom fusion | flops 32768 | bytes 524292 | tf_op jit(solution)/shard_map/scatter-add | solution.py:157
  505.7 12.4 %all-reduce.23 = (f32[2]{0:T(128)S(1)}, f32[2]{0:T(128)S(1)}, f32[2]{0:T(128)S(1)}) all-reduce(f32[2]{0:T(128)S(1)} %maximum_dynamic-update-slice_fusion.1, f32[2]{0:T(128)S(1)} %add_dynamic-update-slice_fusion.4, f32[2]{0:T(128)S(1)} %add_dynamic-update-slice_fusion.2), channel_id=1, replica_groups=mesh['slab_0'=4,'slab_1'=8,'slab_2'=4,'sub'=2] {'sub'}, use_global_device_ids=true, to_apply=%add.11 | all-reduce | flops 6 | bytes 48
  521.5 1.3 collective-permute-start.2
  522.8 1.3 collective-permute-start.3
  524.2 1.3 collective-permute-start.8
  525.5 3.0 collective-permute-start.9
  528.5 3.4 collective-permute-done.3
  532.0 1.3 collective-permute-start.4
  533.3 3.6 collective-permute-start.5
  539.1 2.8 collective-permute-start.10
  544.4 3.8 collective-permute-done.11
  549.5 3.4 collective-permute-start.13
  555.1 5.0 collective-permute-start.14
  562.5 3.8 collective-permute-done.15
  567.7 3.4 collective-permute-start.17
  574.4 4.2 collective-permute-start.18
  580.0 1.8 collective-permute-done.18
  581.7 4.2 collective-permute-done.19
  586.0 1.4 pad_maximum_fusion.38
  588.6 3.0 collective-permute-start.21
  594.8 1.6 fusion.32
  (408 shorter events, 71.8 us)
Async XLA Ops:
  0.6 15.5 %copy-start.5 = (s32[256,128]{1,0:T(8,128)S(1)}, s32[256,128]{1,0:T(8,128)}, u32[]{:S(2)}) copy-start(s32[256,128]{1,0:T(8,128)} %param.9) | copy-start | bytes 393220
  0.6 16.4 %copy-start.8 = (s32[256,8]{0,1:T(8,128)S(1)}, s32[256,8]{0,1:T(8,128)}, u32[]{:S(2)}) copy-start(s32[256,8]{0,1:T(8,128)} %param.10) | copy-start | bytes 24580
  0.7 16.5 %copy-start.7 = (s32[256,128]{1,0:T(8,128)S(1)}, s32[256,128]{1,0:T(8,128)}, u32[]{:S(2)}) copy-start(s32[256,128]{1,0:T(8,128)} %param.11) | copy-start | bytes 393220
  2.4 16.5 %copy-start.12 = (u32[256]{0:T(256)S(1)}, u32[256]{0:T(256)}, u32[]{:S(2)}) copy-start(u32[256]{0:T(256)} %constant.191) | copy-start | bytes 3076
  2.4 18.8 %copy-start = (f32[3,256,128]{2,1,0:T(8,128)S(1)}, f32[3,256,128]{2,1,0:T(8,128)}, u32[]{:S(2)}) copy-start(f32[3,256,128]{2,1,0:T(8,128)} %param.8) | copy-start | bytes 1179652
  2.4 521.7 %collective-permute-start.7 = (f32[2,64,256]{2,1,0:T(8,128)}, f32[2,64,256]{2,1,0:T(8,128)S(1)}, u32[]{:S(2)}, u32[]{:S(2)}) collective-permute-start(f32[2,64,256]{2,1,0:T(8,128)} %get-tuple-element.102), channel_id=1, source_target_pairs={{2,0},{4,2},{6,4},{8,6},{10,8},{12,10},{14,12},{16,14},{18,16},{20... | collective-permute-start | bytes 393224 | tf_op jit(solution)/shard_map/ppermute | solution.py:36
  3.8 516.6 %collective-permute-start.6 = (f32[2,64,256]{2,1,0:T(8,128)}, f32[2,64,256]{2,1,0:T(8,128)}, u32[]{:S(2)}, u32[]{:S(2)}) collective-permute-start(f32[2,64,256]{2,1,0:T(8,128)} %get-tuple-element.103), channel_id=1, source_target_pairs={{0,2},{2,4},{4,6},{6,8},{8,10},{10,12},{12,14},{14,16},{16,18},{18... | collective-permute-start | bytes 393224 | tf_op jit(solution)/shard_map/ppermute | solution.py:35
  12.1 9.1 %collective-permute-start = (f32[4,32,128]{2,0,1:T(4,128)S(1)}, f32[4,32,128]{2,0,1:T(4,128)S(1)}, u32[]{:S(2)}, u32[]{:S(2)}) collective-permute-start(f32[4,32,128]{2,0,1:T(4,128)S(1)} %get-tuple-element.94), channel_id=1, source_target_pairs={{0,2},{2,4},{4,6},{6,8},{8,10},{10,12},{12,14},{14,16},{16,18},{18... | collective-permute-start | bytes 196616 | tf_op jit(solution)/shard_map/ppermute | solution.py:35
  14.8 6.4 %collective-permute-start.1 = (f32[4,32,128]{2,0,1:T(4,128)S(1)}, f32[4,32,128]{2,0,1:T(4,128)S(1)}, u32[]{:S(2)}, u32[]{:S(2)}) collective-permute-start(f32[4,32,128]{2,0,1:T(4,128)S(1)} %get-tuple-element.95), channel_id=1, source_target_pairs={{2,0},{4,2},{6,4},{8,6},{10,8},{12,10},{14,12},{16,14},{18,16},{20... | collective-permute-start | bytes 196616 | tf_op jit(solution)/shard_map/ppermute | solution.py:36
  22.6 265.0 %copy-start.11 = (u32[256]{0:T(256)S(1)}, u32[256]{0:T(256)}, u32[]{:S(2)}) copy-start(u32[256]{0:T(256)} %constant.196) | copy-start | bytes 3076
  22.6 288.3 %copy-start.10 = (u32[256]{0:T(256)S(1)}, u32[256]{0:T(256)}, u32[]{:S(2)}) copy-start(u32[256]{0:T(256)} %constant.201) | copy-start | bytes 3076
  22.6 302.2 %copy-start.9 = (u32[256]{0:T(256)S(1)}, u32[256]{0:T(256)}, u32[]{:S(2)}) copy-start(u32[256]{0:T(256)} %constant.206) | copy-start | bytes 3076
  285.4 235.0 %copy-start.2 = (f32[16,3,16,128]{3,2,1,0:T(8,128)}, f32[16,3,16,128]{3,2,1,0:T(8,128)S(1)}, u32[]{:S(2)}) copy-start(f32[16,3,16,128]{3,2,1,0:T(8,128)S(1)} %get-tuple-element.30) | copy-start | bytes 1179652
  505.6 15.7 %copy-start.4 = (f32[8,64,256]{2,1,0:T(8,128)S(1)}, f32[8,64,256]{2,1,0:T(8,128)}, u32[]{:S(2)}) copy-start(f32[8,64,256]{2,1,0:T(8,128)} %param.12) | copy-start | bytes 1572868
  505.6 15.7 %copy-start.6 = (f32[8,64,256]{2,1,0:T(8,128)S(1)}, f32[8,64,256]{2,1,0:T(8,128)}, u32[]{:S(2)}) copy-start(f32[8,64,256]{2,1,0:T(8,128)} %param.13) | copy-start | bytes 1572868
  521.5 7.0 %collective-permute-start.2 = (f32[2,2,64,256]{3,2,1,0:T(8,128)S(1)}, f32[2,2,64,256]{3,2,1,0:T(8,128)S(1)}, u32[]{:S(2)}, u32[]{:S(2)}) collective-permute-start(f32[2,2,64,256]{3,2,1,0:T(8,128)S(1)} %get-tuple-element.84), channel_id=1, source_target_pairs={{0,2},{2,4},{4,6},{6,8},{8,10},{10,12},{12,14},{14,16},{16,18},{18... | collective-permute-start | bytes 786440 | tf_op jit(solution)/shard_map/ppermute | solution.py:35
  522.8 9.1 %collective-permute-start.3 = (f32[2,2,64,256]{3,2,1,0:T(8,128)S(1)}, f32[2,2,64,256]{3,2,1,0:T(8,128)S(1)}, u32[]{:S(2)}, u32[]{:S(2)}) collective-permute-start(f32[2,2,64,256]{3,2,1,0:T(8,128)S(1)} %get-tuple-element.85), channel_id=1, source_target_pairs={{2,0},{4,2},{6,4},{8,6},{10,8},{12,10},{14,12},{16,14},{18,16},{20... | collective-permute-start | bytes 786440 | tf_op jit(solution)/shard_map/ppermute | solution.py:36
  524.2 12.7 %collective-permute-start.8 = (f32[12,2,256]{2,1,0:T(2,128)S(1)}, f32[12,2,256]{2,1,0:T(2,128)S(1)}, u32[]{:S(2)}, u32[]{:S(2)}) collective-permute-start(f32[12,2,256]{2,1,0:T(2,128)S(1)} %get-tuple-element.92), channel_id=1, source_target_pairs={{0,1},{2,3},{4,5},{6,7},{8,9},{10,11},{12,13},{14,15},{16,17},{18,... | collective-permute-start | bytes 73736 | tf_op jit(solution)/shard_map/ppermute | solution.py:35
  525.5 11.4 %collective-permute-start.9 = (f32[12,2,256]{2,1,0:T(2,128)S(1)}, f32[12,2,256]{2,1,0:T(2,128)S(1)}, u32[]{:S(2)}, u32[]{:S(2)}) collective-permute-start(f32[12,2,256]{2,1,0:T(2,128)S(1)} %get-tuple-element.93), channel_id=1, source_target_pairs={{1,0},{3,2},{5,4},{7,6},{9,8},{11,10},{13,12},{15,14},{17,16},{19,... | collective-permute-start | bytes 73736 | tf_op jit(solution)/shard_map/ppermute | solution.py:36
  532.0 5.1 collective-permute-start.4
  533.3 4.3 collective-permute-start.5
  539.1 5.2 collective-permute-start.10
  541.9 6.3 %collective-permute-start.11 = (f32[2,64,256]{2,1,0:T(8,128)S(1)}, f32[2,64,256]{2,1,0:T(8,128)S(1)}, u32[]{:S(2)}, u32[]{:S(2)}) collective-permute-start(f32[2,64,256]{2,1,0:T(8,128)S(1)} %get-tuple-element.101), channel_id=1, source_target_pairs={{2,0},{4,2},{6,4},{8,6},{10,8},{12,10},{14,12},{16,14},{18,16},{20... | collective-permute-start | bytes 393224 | tf_op jit(solution)/shard_map/ppermute | solution.py:36
  548.2 4.7 collective-permute-start.12
  549.5 4.2 collective-permute-start.13
  555.1 7.5 %collective-permute-start.14 = (f32[2,64,256]{2,1,0:T(8,128)S(1)}, f32[2,64,256]{2,1,0:T(8,128)S(1)}, u32[]{:S(2)}, u32[]{:S(2)}) collective-permute-start(f32[2,64,256]{2,1,0:T(8,128)S(1)} %get-tuple-element.98), channel_id=1, source_target_pairs={{0,2},{2,4},{4,6},{6,8},{8,10},{10,12},{12,14},{14,16},{16,18},{18... | collective-permute-start | bytes 393224 | tf_op jit(solution)/shard_map/ppermute | solution.py:35
  560.0 6.3 %collective-permute-start.15 = (f32[2,64,256]{2,1,0:T(8,128)S(1)}, f32[2,64,256]{2,1,0:T(8,128)S(1)}, u32[]{:S(2)}, u32[]{:S(2)}) collective-permute-start(f32[2,64,256]{2,1,0:T(8,128)S(1)} %get-tuple-element.99), channel_id=1, source_target_pairs={{2,0},{4,2},{6,4},{8,6},{10,8},{12,10},{14,12},{16,14},{18,16},{20... | collective-permute-start | bytes 393224 | tf_op jit(solution)/shard_map/ppermute | solution.py:36
  566.4 6.6 %collective-permute-start.16 = (f32[12,2,256]{2,1,0:T(2,128)S(1)}, f32[12,2,256]{2,1,0:T(2,128)S(1)}, u32[]{:S(2)}, u32[]{:S(2)}) collective-permute-start(f32[12,2,256]{2,1,0:T(2,128)S(1)} %get-tuple-element.88), channel_id=1, source_target_pairs={{0,1},{2,3},{4,5},{6,7},{8,9},{10,11},{12,13},{14,15},{16,17},{18,... | collective-permute-start | bytes 73736 | tf_op jit(solution)/shard_map/ppermute | solution.py:35
  567.7 5.3 collective-permute-start.17
  574.0 5.9 copy-start.3
  574.4 17.3 %copy-start.1 = (f32[3,256,128]{2,1,0:T(8,128)S(1)}, f32[3,256,128]{2,1,0:T(8,128)}, u32[]{:S(2)}) copy-start(f32[3,256,128]{2,1,0:T(8,128)} %param.8) | copy-start | bytes 1179652
  574.4 7.3 %collective-permute-start.18 = (f32[2,64,256]{2,1,0:T(8,128)S(1)}, f32[2,64,256]{2,1,0:T(8,128)S(1)}, u32[]{:S(2)}, u32[]{:S(2)}) collective-permute-start(f32[2,64,256]{2,1,0:T(8,128)S(1)} %get-tuple-element.96), channel_id=1, source_target_pairs={{0,2},{2,4},{4,6},{6,8},{8,10},{10,12},{12,14},{14,16},{16,18},{18... | collective-permute-start | bytes 393224 | tf_op jit(solution)/shard_map/ppermute | solution.py:35
  578.6 7.4 %collective-permute-start.19 = (f32[2,64,256]{2,1,0:T(8,128)S(1)}, f32[2,64,256]{2,1,0:T(8,128)}, u32[]{:S(2)}, u32[]{:S(2)}) collective-permute-start(f32[2,64,256]{2,1,0:T(8,128)S(1)} %get-tuple-element.97), channel_id=1, source_target_pairs={{2,0},{4,2},{6,4},{8,6},{10,8},{12,10},{14,12},{16,14},{18,16},{20... | collective-permute-start | bytes 393224 | tf_op jit(solution)/shard_map/ppermute | solution.py:36
  587.3 6.4 %collective-permute-start.20 = (f32[12,2,256]{2,1,0:T(2,128)}, f32[12,2,256]{2,1,0:T(2,128)S(1)}, u32[]{:S(2)}, u32[]{:S(2)}) collective-permute-start(f32[12,2,256]{2,1,0:T(2,128)} %get-tuple-element.86), channel_id=1, source_target_pairs={{0,1},{2,3},{4,5},{6,7},{8,9},{10,11},{12,13},{14,15},{16,17},{18,... | collective-permute-start | bytes 73736 | tf_op jit(solution)/shard_map/ppermute | solution.py:35
  588.6 5.1 collective-permute-start.21
where the time goes:
time: 609 us; the launch traced here: 599 us
  other arithmetic  423 us (69%)
  starting transfers between devices  51.9 us (9%)
  blocking collectives  50.3 us (8%)
  local copies, waits for them, and re-layouts  42.2 us (7%)
  waiting for transfers between devices  20.8 us (3%)
  between operations  7.91 us (1%)
    reduce_sum x16, other arithmetic, pair_forces(): jnp.sum(weight * delta_x, -1)  226 us
    scatter-add x1, other arithmetic, body(): cell_count = jnp.zeros((size_x * size_y * size_z,), jnp.float32).at[local...  171 us
    unnamed x4, blocking collectives  50.3 us
    ppermute x11, starting transfers between devices, with_halo(): before = lax.ppermute(last, axis, up)  27.7 us
    ppermute x11, starting transfers between devices, with_halo(): after = lax.ppermute(initial, axis, down)  24.3 us
    ppermute x11, waiting for transfers between devices, with_halo(): after = lax.ppermute(initial, axis, down)  16.6 us
    slice x16, local copies, waits for them, and re-layouts, pair_forces(): others[3][:, None, :]  13.8 us
  transfers between devices with their start and end apart: 22, of which 9 were waited for; matrix products, arithmetic and copies ran while one was open for 76% of the time, Pallas kernels for 0%

commit v1 on v0

v1 whole, which is shorter than its diff:
```python
import jax
import jax.numpy as jnp
from jax import lax
from jax.experimental import pallas as pl
from jax.experimental.pallas import tpu as pltpu
from jax.sharding import Mesh
from jax.sharding import PartitionSpec as P

TILE = 128
NB = 8
GHOST = 32
SWEEPS = 8
SLAB = ("slab_0", "slab_1", "slab_2")
SLAB_SUB = ("slab_0", "slab_1", "slab_2", "sub")

SOFTENING = 0.01
REPEL_RADIUS = 2.0
ADHERE_RADIUS = 3.0
REPEL_STRENGTH = 0.05
ADHERE_STRENGTH = 0.02
SPEED_LIMIT = 0.2
SPEED_EPSILON = 1e-06
SUBSTRATE_STEP = 0.5
DECAY_RATE = 0.1
DIFFUSION_NUMBER = 2.0
UPTAKE_SCALE = 0.25

FEATURES = 32
FAR = float(2**20)
REPEL_FACTOR = REPEL_STRENGTH / REPEL_RADIUS**2
ADHERE_RATIO = ADHERE_STRENGTH / ADHERE_RADIUS**2 / REPEL_FACTOR
F32 = jnp.float32
BF16 = jnp.bfloat16
VMEM = pltpu.VMEM
VMEM_LIMIT = 60 * 1024 * 1024


def split(x):
    high = x.astype(BF16).astype(F32)
    rest = x - high
    middle = rest.astype(BF16).astype(F32)
    return high, middle, rest - middle


def count_kernel(sub_ref, voxel_ref, state_ref, substrate_ref, secretion_ref, own_ref, edge_ref, count):
    size_x, size_y, size_z = substrate_ref.shape
    grid_y = size_y * 2
    rows = size_x * size_y
    group = 8
    row_id = lax.broadcasted_iota(jnp.int32, (rows, TILE), 0)
    z_id = lax.broadcasted_iota(jnp.int32, (size_z, TILE), 0)
    count[...] = jnp.zeros_like(count)

    def step(g, carry):
        at = pl.multiple_of(g * group, group)
        voxel = voxel_ref[pl.ds(at, group), :]
        live = state_ref[pl.ds(at, group), :] == 1
        z = voxel % size_z
        column = voxel // size_z % size_y
        row = (voxel // (size_z * grid_y) % size_x) * size_y + column
        row = jnp.where(live, row, -1)
        total = None
        for pair in range(0, group, 2):
            left = []
            right = []
            for i in (pair, pair + 1):
                left.append(jnp.where(row_id == row[i : i + 1, :], 1.0, 0.0).astype(BF16))
                right.append(jnp.where(z_id == z[i : i + 1, :], 1.0, 0.0).astype(BF16))
            part = lax.dot_general(
                jnp.concatenate(left, 1),
                jnp.concatenate(right, 1),
                (((1,), (1,)), ((), ())),
                preferred_element_type=F32,
            )
            total = part if total is None else total + part
        count[...] += total
        return carry

    lax.fori_loop(0, voxel_ref.shape[0] // group, step, 0)
    own_ref[0, :, 8 : 8 + size_y, :] = substrate_ref[...]
    own_ref[1, :, 8 : 8 + size_y, :] = secretion_ref[...]
    own_ref[2, :, 8 : 8 + size_y, :] = count[...].reshape(size_x, size_y, size_z)
    edge = pl.multiple_of(8 + (1 - sub_ref[0]) * (size_y - 8), 8)
    edge_ref[...] = own_ref[:, :, pl.ds(edge, 8), :]


def force_kernel(
    ids_ref, own_ref, before_ref, after_ref, velocity_ref, stats_ref,
    features, adhere, weights, left_rows, right_rows, even, odd,
):
    tiles = own_ref.shape[1]
    center = lax.broadcasted_iota(jnp.int32, (FEATURES, TILE), 0)
    ratio = split(jnp.full((FEATURES, TILE), ADHERE_RATIO, F32))
    ratio_rows = jnp.where(
        center == 25, ratio[0], jnp.where(center == 26, ratio[1], jnp.where(center == 27, ratio[2], 0.0))
    ).astype(BF16)
    zero = jnp.zeros((8, TILE), F32)
    one = jnp.ones((8, TILE), F32)

    def put_left(source, at, target):
        state = source[3, pl.ds(at, 8), :]
        live = jnp.where(state == 1.0, 1.0, 0.0)
        vacant = jnp.where(state > 0.5, 0.0, FAR)
        norm = zero
        rows = []
        for axis in range(3):
            value = source[axis, pl.ds(at, 8), :]
            norm = norm + value * value
            high, middle, low = split(value)
            rows += [high, high, high, middle, middle, low]
        rows += [one, one, one]
        rows += list(split(norm))
        rows += [vacant, live, live, live]
        for k, row in enumerate(rows):
            left_rows[k * 8 : k * 8 + 8, :] = row
        for i in range(8):
            block = left_rows[pl.ds(i, FEATURES, stride=8), :]
            turned = block.T.astype(BF16)
            features[target + i] = turned
            adhere[target + i] = jnp.dot(turned, ratio_rows, preferred_element_type=F32)

    def put_right(at):
        norm = jnp.full((8, TILE), SOFTENING, F32)
        for axis in range(3):
            value = own_ref[axis, pl.ds(at, 8), :]
            norm = norm + value * value
            pieces = split(value)
            high, middle, low = [-2.0 * piece for piece in pieces]
            for k, row in enumerate([high, middle, low, high, middle, high]):
                n = axis * 6 + k
                right_rows[0, n * 8 : n * 8 + 8, :] = row
            for k in range(3):
                n = 18 + k
                right_rows[axis + 1, n * 8 : n * 8 + 8, :] = pieces[k]
        for k, row in enumerate(split(norm)):
            n = 18 + k
            right_rows[0, n * 8 : n * 8 + 8, :] = row
        for i in range(8):
            for part in range(4):
                weights[at + i, :, part * TILE : part * TILE + TILE] = right_rows[
                    part, pl.ds(i, FEATURES, stride=8), :
                ].astype(BF16)

    left_rows[...] = jnp.zeros_like(left_rows)
    right_rows[...] = jnp.zeros_like(right_rows)
    for n in range(21, 25):
        right_rows[0, n * 8 : n * 8 + 8, :] = one
    for axis in range(3):
        for k in (0, 3, 5):
            n = axis * 6 + k
            right_rows[axis + 1, n * 8 : n * 8 + 8, :] = -one

    def ghosts(g, carry):
        at = pl.multiple_of(g * 8, 8)
        put_left(before_ref, at, at)
        put_left(after_ref, at, at + GHOST + tiles)
        return carry

    def owned(g, carry):
        at = pl.multiple_of(g * 8, 8)
        put_left(own_ref, at, at + GHOST)
        put_right(at)
        return carry

    lax.fori_loop(0, GHOST // 8, ghosts, 0)
    lax.fori_loop(0, tiles // 8, owned, 0)

    def products(tile, j, target):
        other = ids_ref[tile * NB + j]
        target[j * TILE : (j + 1) * TILE, :] = jnp.dot(
            features[other], weights[tile], preferred_element_type=F32
        )

    def pairs(tile, j, source, reach, total):
        other = ids_ref[tile * NB + j]
        chunk = 32
        for c in range(0, TILE, chunk):
            rows = slice(j * TILE + c, j * TILE + c + chunk)
            square = source[rows, 0:TILE]
            inverse = lax.rsqrt(square)
            distance = square * inverse
            near = jnp.maximum(REPEL_RADIUS - distance, 0.0)
            far = jnp.maximum(reach - distance, 0.0)
            weight = (near * near - adhere[other, c : c + chunk, :] * (far * far)) * inverse
            for axis in range(3):
                term = weight * source[rows, (axis + 1) * TILE : (axis + 2) * TILE]
                total[axis] = total[axis] + jnp.sum(term.reshape(chunk // 8, 8, TILE), 0)
        return total

    def one_tile(tile, following, source, target):
        live = own_ref[3, pl.ds(tile, 1), :] == 1.0
        reach = jnp.broadcast_to(jnp.where(live, ADHERE_RADIUS, -1.0), (32, TILE))
        total = [zero, zero, zero]
        for j in range(NB):
            products(following, j, target)
            total = pairs(tile, j, source, reach, total)
        for axis in range(3):
            velocity_ref[axis, pl.ds(tile, 1), :] = jnp.sum(total[axis], 0, keepdims=True)

    for j in range(NB):
        products(0, j, even)

    def two_tiles(i, carry):
        tile = i * 2
        one_tile(tile, tile + 1, even, odd)
        one_tile(tile + 1, jnp.minimum(tile + 2, tiles - 1), odd, even)
        return carry

    lax.fori_loop(0, tiles // 2, two_tiles, 0)

    state = own_ref[3]
    scale = jnp.where(state > 0.5, REPEL_FACTOR, 0.0)
    speed = jnp.zeros((tiles, TILE), F32)
    for axis in range(3):
        value = velocity_ref[axis] * scale
        velocity_ref[axis] = value
        speed = speed + value * value
    fastest = jnp.max(jnp.sqrt(speed))
    live = jnp.sum(jnp.where(state == 1.0, 1.0, 0.0))
    necrotic = jnp.sum(jnp.where(state == 2.0, 1.0, 0.0))
    lane = lax.broadcasted_iota(jnp.int32, stats_ref.shape, 2)
    stats_ref[...] = jnp.where(lane == 0, fastest, jnp.where(lane == 1, live, necrotic))


def sweep_kernel(
    where_ref, stats_ref, position_ref, velocity_ref, before_ref, own_ref, after_ref,
    new_position_ref, new_substrate_ref, fraction_ref, even, odd, constant, factor,
):
    _, size_x, rows, size_z = own_ref.shape
    size_y = rows - 16
    halves = size_z // TILE
    slab, slabs, subs = where_ref[0], where_ref[1], where_ref[2]
    sub = where_ref[3]
    stats = stats_ref[...]
    lane = lax.broadcasted_iota(jnp.int32, stats.shape, 2)
    fastest = jnp.max(jnp.where(lane == 0, stats, 0.0))
    live = jnp.sum(jnp.where(lane == 1, stats, 0.0))
    necrotic = jnp.sum(jnp.where(lane == 2, stats, 0.0))
    grid_total = size_x * slabs * size_y * subs * size_z
    live_row = jnp.full((8, TILE), live, F32)
    per_cell = UPTAKE_SCALE * jnp.full((8, TILE), grid_total.astype(F32), F32) / live_row
    fraction = jnp.full((8, TILE), necrotic, F32) / (live_row + necrotic)
    fraction_ref[0] = fraction[0, 0]
    step = SPEED_LIMIT / (jnp.full((8, TILE), fastest, F32) + SPEED_EPSILON)
    step_row = step[0:1, :]
    for axis in range(3):
        new_position_ref[axis] = position_ref[axis] + step_row * velocity_ref[axis]
    per_row = per_cell[0:1, :]
    y = lax.broadcasted_iota(jnp.int32, (rows, TILE), 0)
    lowest = jnp.where(sub == 0, 8, 0)
    inside = (y >= lowest) & (y < lowest + size_y + 8)

    def margins(x, carry):
        for field in (even, odd):
            for half in range(halves):
                field[x, half, 0:8, :] = jnp.zeros((8, TILE), F32)
                field[x, half, 8 + rows : 16 + rows, :] = jnp.zeros((8, TILE), F32)
        return carry

    lax.fori_loop(0, 3 * size_x, margins, 0)

    for source, at, present in (
        (before_ref, 0, slab > 0),
        (own_ref, size_x, slab >= 0),
        (after_ref, 2 * size_x, slab < slabs - 1),
    ):
        usable = inside & present

        def fill(x, carry, source=source, at=at, usable=usable):
            base = 1.0 + SUBSTRATE_STEP * DECAY_RATE + 6.0 * DIFFUSION_NUMBER
            for half in range(halves):
                lanes = slice(half * TILE, half * TILE + TILE)
                substrate = source[0, x, :, lanes]
                right_side = substrate + SUBSTRATE_STEP * source[1, x, :, lanes]
                inverse = 1.0 / (base + per_row * source[2, x, :, lanes])
                even[at + x, half, 8 : 8 + rows, :] = jnp.where(usable, substrate, 0.0)
                constant[at + x, half] = jnp.where(usable, right_side * inverse, 0.0)
                factor[at + x, half] = jnp.where(usable, DIFFUSION_NUMBER * inverse, 0.0)
            return carry

        lax.fori_loop(0, size_x, fill, 0)

    low_lane = lax.broadcasted_iota(jnp.int32, (rows, TILE), 1) == 0
    high_lane = lax.broadcasted_iota(jnp.int32, (rows, TILE), 1) == TILE - 1
    here = slice(8, 8 + rows)
    for k in range(SWEEPS):
        source, target = (even, odd) if k % 2 == 0 else (odd, even)
        final = k == SWEEPS - 1

        def sweep(x, carry, source=source, target=target, final=final):
            middle = [source[x, half, here, :] for half in range(halves)]
            right = [pltpu.roll(value, 1, 1) for value in middle]
            left = [pltpu.roll(value, TILE - 1, 1) for value in middle]
            for half in range(halves):
                total = source[x - 1, half, here, :] + source[x + 1, half, here, :]
                total = total + source[x, half, 7 : 7 + rows, :]
                total = total + source[x, half, 9 : 9 + rows, :]
                lower = right[half - 1] if half > 0 else 0.0
                upper = left[half + 1] if half < halves - 1 else 0.0
                total = total + jnp.where(low_lane, lower, right[half])
                total = total + jnp.where(high_lane, upper, left[half])
                value = constant[x, half] + factor[x, half] * total
                if final:
                    new_substrate_ref[x - size_x, :, half * TILE : half * TILE + TILE] = value[8 : 8 + size_y]
                else:
                    target[x, half, here, :] = value
            return carry

        lax.fori_loop(k + 1, 3 * size_x - k - 1, sweep, 0)


WHOLE = pl.BlockSpec(memory_space=pltpu.VMEM)
SCALAR = pl.BlockSpec(memory_space=pltpu.SMEM)


def counts(sub_index, voxel, state, substrate, secretion):
    size_x, size_y, size_z = substrate.shape
    return pl.pallas_call(
        count_kernel,
        out_shape=(
            jax.ShapeDtypeStruct((3, size_x, size_y + 16, size_z), F32),
            jax.ShapeDtypeStruct((3, size_x, 8, size_z), F32),
        ),
        in_specs=[SCALAR] + [WHOLE] * 4,
        out_specs=(WHOLE, WHOLE),
        scratch_shapes=[VMEM((size_x * size_y, size_z), F32)],
        compiler_params=pltpu.CompilerParams(vmem_limit_bytes=VMEM_LIMIT),
        cost_estimate=pl.CostEstimate(flops=9 * 10**9, bytes_accessed=4 * 10**6, transcendentals=0),
        name="counts",
    )(sub_index, voxel, state, substrate, secretion)


def forces(local_ids, codes, ghost_before, ghost_after, devices):
    tiles_dev = codes.shape[1]
    all_tiles = tiles_dev + 2 * GHOST
    return pl.pallas_call(
        force_kernel,
        out_shape=(
            jax.ShapeDtypeStruct((3, tiles_dev, TILE), F32),
            jax.ShapeDtypeStruct((devices, 1, TILE), F32),
        ),
        in_specs=[SCALAR] + [WHOLE] * 3,
        out_specs=(WHOLE, WHOLE),
        scratch_shapes=[
            VMEM((all_tiles, TILE, FEATURES), BF16),
            VMEM((all_tiles, TILE, TILE), F32),
            VMEM((tiles_dev, FEATURES, 4 * TILE), BF16),
            VMEM((FEATURES * 8, TILE), F32),
            VMEM((4, FEATURES * 8, TILE), F32),
            VMEM((NB * TILE, 4 * TILE), F32),
            VMEM((NB * TILE, 4 * TILE), F32),
        ],
        compiler_params=pltpu.CompilerParams(vmem_limit_bytes=VMEM_LIMIT),
        cost_estimate=pl.CostEstimate(flops=10**11, bytes_accessed=10**6, transcendentals=0),
        name="forces",
    )(local_ids, codes, ghost_before, ghost_after)


def sweeps(location, stats, position, velocity, before, own, after):
    _, size_x, rows, size_z = own.shape
    planes = (3 * size_x, size_z // TILE)
    return pl.pallas_call(
        sweep_kernel,
        out_shape=(
            jax.ShapeDtypeStruct(position.shape, F32),
            jax.ShapeDtypeStruct((size_x, rows - 16, size_z), F32),
            jax.ShapeDtypeStruct((1,), F32),
        ),
        in_specs=[SCALAR] + [WHOLE] * 6,
        out_specs=(WHOLE, WHOLE, SCALAR),
        scratch_shapes=[
            VMEM(planes + (rows + 16, TILE), F32),
            VMEM(planes + (rows + 16, TILE), F32),
            VMEM(planes + (rows, TILE), F32),
            VMEM(planes + (rows, TILE), F32),
        ],
        compiler_params=pltpu.CompilerParams(vmem_limit_bytes=VMEM_LIMIT),
        cost_estimate=pl.CostEstimate(flops=10**9, bytes_accessed=8 * 10**6, transcendentals=0),
        name="sweeps",
    )(location, stats, position, velocity, before, own, after)


def body(position, state, neighbours, voxel, substrate, secretion):
    tiles_dev = position.shape[1]
    sub_count = lax.axis_size("sub")
    slab_count = lax.axis_size(SLAB)
    slab_index = lax.axis_index(SLAB)
    sub_index = lax.axis_index("sub")
    device = slab_index * sub_count + sub_index
    size_y = substrate.shape[1]
    up = [(i, i + 1) for i in range(slab_count - 1)]
    down = [(i + 1, i) for i in range(slab_count - 1)]

    codes = jnp.concatenate([position, state.astype(F32)[None]], 0)
    ghost_before = lax.ppermute(codes[:, tiles_dev - GHOST :], SLAB, up)
    ghost_after = lax.ppermute(codes[:, :GHOST], SLAB, down)

    own, edge = counts(sub_index.reshape(1), voxel, state, substrate, secretion)
    other = lax.ppermute(edge, "sub", [(0, 1), (1, 0)])
    own = lax.dynamic_update_slice(own, other, (0, 0, (1 - sub_index) * (size_y + 8), 0))
    field_before = lax.ppermute(own, SLAB, up)
    field_after = lax.ppermute(own, SLAB, down)

    first_tile = device * tiles_dev
    local_ids = jnp.where(
        neighbours < first_tile,
        neighbours - (first_tile - sub_count * tiles_dev) - (tiles_dev - GHOST),
        jnp.where(
            neighbours >= first_tile + tiles_dev,
            GHOST + tiles_dev + neighbours - (first_tile + sub_count * tiles_dev),
            GHOST + neighbours - first_tile,
        ),
    ).reshape(-1)
    velocity, stats = forces(local_ids, codes, ghost_before, ghost_after, slab_count * sub_count)
    stats = lax.all_to_all(stats, SLAB_SUB, 0, 0, tiled=True)
    location = jnp.stack([slab_index, jnp.int32(slab_count), jnp.int32(sub_count), sub_index])
    new_position, new_substrate, fraction = sweeps(
        location, stats, position, velocity, field_before, own, field_after
    )
    return (new_position, new_substrate, fraction.reshape(()))


def solution(mesh):
    finer = Mesh(
        mesh.devices.reshape(4, 8, 4, mesh.shape["sub"]), ("slab_0", "slab_1", "slab_2", "sub")
    )
    placed = (
        P(None, SLAB_SUB, None),
        P(SLAB_SUB, None),
        P(SLAB_SUB, None),
        P(SLAB_SUB, None),
        P(SLAB, "sub", None),
        P(SLAB, "sub", None),
    )
    return jax.shard_map(
        body,
        mesh=finer,
        in_specs=placed,
        out_specs=(P(None, SLAB_SUB, None), P(SLAB, "sub", None), P()),
        check_vma=False,
    )
```

time: 609 us -> 209 us (0.34); the launches traced: 599 us -> 208 us
  other arithmetic: 423 us -> 3.2 us
  Pallas kernels: 0 us -> 154 us
  blocking collectives: 50.3 us -> 0 us
  local copies, waits for them, and re-layouts: 42.2 us -> 4.07 us
  starting transfers between devices: 51.9 us -> 34.3 us
  waiting for transfers between devices: 20.8 us -> 12.2 us
  between operations: 7.91 us -> 0.72 us
    reduce_sum x19 -> x0, other arithmetic: 229 us -> none  [the longest x16 226 us: pair_forces(): jnp.sum(weight * delta_x, -1)]
    scatter-add x1 -> x0, other arithmetic: 171 us -> none  [body(): cell_count = jnp.zeros((size_x * size_y * size_z,), jnp.float32).at[local...]
    pallas_call x0 -> x3, Pallas kernels: none -> 154 us  [the longest x1 116 us: forces(): pl.pallas_call(force_kernel, out_shape=(jax.ShapeDtypeStruct((3, tiles_de...]
    unnamed x4 -> x0, blocking collectives: 50.3 us -> none
    ppermute x22 -> x5, starting transfers between devices: 51.9 us -> 15.6 us  [the longest x1 5.3 us: body(): field_before = lax.ppermute(own, SLAB, up)]
    ppermute x22 -> x5, waiting for transfers between devices: 20.8 us -> 0.01 us  [the longest x1 0.01 us: body(): ghost_after = lax.ppermute(codes[:, :GHOST], SLAB, down)]
    all_to_all x0 -> x1, starting transfers between devices: none -> 18.7 us  [body(): stats = lax.all_to_all(stats, SLAB_SUB, 0, 0, tiled=True)]
    slice x31 -> x0, local copies, waits for them, and re-layouts: 17.2 us -> none  [the longest x16 13.8 us: pair_forces(): others[3][:, None, :]]
  transfers between devices with their start and end apart: 22 -> 6, of which waited for: 9 -> 1; matrix products, arithmetic and copies ran while one was open for 76% -> 1% of each run, Pallas kernels for 0% -> 65%
where the time goes in v1:
time: 209 us; the launch traced here: 208 us
  Pallas kernels  154 us (74%)
  starting transfers between devices  34.3 us (16%)
  waiting for transfers between devices  12.2 us (6%)
  local copies, waits for them, and re-layouts  4.07 us (2%)
  other arithmetic  3.2 us (2%)
    pallas_call x1, Pallas kernels, forces(): pl.pallas_call(force_kernel, out_shape=(jax.ShapeDtypeStruct((3, tiles_de...  116 us
    pallas_call x1, Pallas kernels, sweeps(): pl.pallas_call(sweep_kernel, out_shape=(jax.ShapeDtypeStruct(position.sha...  19 us
    pallas_call x1, Pallas kernels, counts(): pl.pallas_call(count_kernel, out_shape=(jax.ShapeDtypeStruct((3, size_x,...  18.7 us
    all_to_all x1, starting transfers between devices, body(): stats = lax.all_to_all(stats, SLAB_SUB, 0, 0, tiled=True)  18.7 us
    all_to_all x1, waiting for transfers between devices, body(): stats = lax.all_to_all(stats, SLAB_SUB, 0, 0, tiled=True)  12.2 us
    ppermute x1, starting transfers between devices, body(): field_before = lax.ppermute(own, SLAB, up)  5.3 us
    ppermute x1, starting transfers between devices, body(): ghost_before = lax.ppermute(codes[:, tiles_dev - GHOST:], SLAB, up)  4.65 us
  transfers between devices with their start and end apart: 6, of which 1 were waited for; matrix products, arithmetic and copies ran while one was open for 1% of the time, Pallas kernels for 65%

profile of v1, /device:TPU:1, one launch (start us, length us, event | category | flops | bytes accessed | tf_op | source)
XLA Modules:
  0.0 208.4 jit_solution(8250323285793906712)
XLA Ops:
  0.6 0.9 convert_bitcast_fusion
  1.5 0.8 fusion.1
  2.4 1.3 collective-permute-start.1
  3.7 4.7 %collective-permute-start = (f32[4,32,128]{2,1,0:T(8,128)S(1)}, f32[4,32,128]{2,1,0:T(8,128)S(1)}, u32[]{:S(2)}, u32[]{:S(2)}) collective-permute-start(f32[4,32,128]{2,1,0:T(8,128)S(1)} %get-tuple-element.18), channel_id=1, source_target_pairs={{0,2},{2,4},{4,6},{6,8},{8,10},{10,12},{12,14},{14,16},{16,18},{18... | collective-permute-start | bytes 196616 | tf_op jit(solution)/shard_map/ppermute | solution.py:395
  8.4 0.0 copy-start.3
  8.4 0.0 copy-start
  8.4 18.7 %counts.1 = (f32[3,8,80,256]{3,2,1,0:T(8,128)}, f32[3,8,8,256]{3,2,1,0:T(8,128)}) custom-call(s32[1]{0:T(128)} %bitcast.1.sub_ref, s32[256,128]{1,0:T(8,128)} %voxel_ref.1, s32[256,128]{1,0:T(8,128)} %state_ref.1, f32[8,64,256]{2,1,0:T(8,128)} %substrate_ref.1, f32[8,64,256]{2,1,0:T(8,128)} %secretion_ref.1), custom_call_target="tpu_custom_call" | custom-call | flops 8999999488 | bytes 4000000 | tf_op jit(solution)/shard_map/counts/pallas_call | solution.py:318
  27.1 3.1 %collective-permute-start.2 = (f32[3,8,8,256]{3,2,1,0:T(8,128)}, f32[3,8,8,256]{3,2,1,0:T(8,128)S(1)}, u32[]{:S(2)}, u32[]{:S(2)}) collective-permute-start(f32[3,8,8,256]{3,2,1,0:T(8,128)} %get-tuple-element.13), channel_id=1, source_target_pairs={{0,1},{1,0},{2,3},{3,2},{4,5},{5,4},{6,7},{7,6},{8,9},{9,8},{10,11... | collective-permute-start | bytes 589832 | tf_op jit(solution)/shard_map/ppermute | solution.py:399
  30.2 0.0 copy-done.3
  30.2 0.1 copy.9
  30.3 0.7 reshape.13.ids_ref
  31.0 0.0 copy-done
  31.0 0.8 pad_maximum_fusion.own_ref
  31.9 0.0 collective-permute-done.2
  31.9 0.7 constant_dynamic-update-slice_fusion.own_ref
  32.6 1.3 collective-permute-start.4
  33.9 5.3 %collective-permute-start.3 = (f32[3,8,80,256]{3,2,1,0:T(8,128)}, f32[3,8,80,256]{3,2,1,0:T(8,128)}, u32[]{:S(2)}, u32[]{:S(2)}) collective-permute-start(f32[3,8,80,256]{3,2,1,0:T(8,128)} %constant_dynamic-update-slice_fusion.own_ref), channel_id=1, source_target_pairs={{0,2},{2,4},{4,6},{6,8},{8,10},{10,12},{12,14},{14,16},{16,18},{18... | collective-permute-start | bytes 5898248 | tf_op jit(solution)/shard_map/ppermute | solution.py:401
  39.2 0.0 collective-permute-done.1.after_ref
  39.2 0.0 copy-start.4
  39.2 0.0 collective-permute-done.before_ref
  39.2 0.6 copy-done.4
  39.8 0.0 copy-start.5
  39.8 0.6 copy-done.5
  40.4 116.3 %forces.1 = (f32[3,256,128]{2,1,0:T(8,128)}, f32[256,1,128]{2,1,0:T(1,128)}) custom-call(s32[2048]{0:T(1024)} %reshape.13.ids_ref, f32[4,256,128]{2,1,0:T(8,128)} %pad_maximum_fusion.own_ref, f32[4,32,128]{2,1,0:T(8,128)} %copy-done.5, f32[4,32,128]{2,1,0:T(8,128)} %copy-done.4), custom_call_target="tpu_custom_call" | custom-call | flops 99999997952 | bytes 1000000 | tf_op jit(solution)/shard_map/forces/pallas_call | solution.py:336
  156.7 18.7 %all-to-all-start = ((f32[256,1,128]{2,1,0:T(1,128)}), f32[256,1,128]{2,1,0:T(1,128)S(1)}, u32[]{:S(2)}, u32[]{:S(2)}) async-start(f32[256,1,128]{2,1,0:T(1,128)} %get-tuple-element.10), calls=%async_computation | async-start | bytes 262144 | tf_op jit(solution)/shard_map/all_to_all | solution.py:415
  175.3 0.6 pad_add_fusion.where_ref
  176.0 12.2 %all-to-all-done.stats_ref = f32[256,1,128]{2,1,0:T(1,128)S(1)} async-done(((f32[256,1,128]{2,1,0:T(1,128)}), f32[256,1,128]{2,1,0:T(1,128)S(1)}, u32[]{:S(2)}, u32[]{:S(2)}) %all-to-all-start) | async-done | bytes 131104 | tf_op jit(solution)/shard_map/all_to_all | solution.py:415
  188.1 0.0 copy-start.2
  188.1 0.0 collective-permute-done.4.after_ref
  188.1 0.0 copy-start.1
  188.1 0.0 collective-permute-done.3.before_ref
  188.1 0.6 copy-done.2
  188.8 0.7 copy-done.1
  189.4 19.0 %sweeps.1 = (f32[3,256,128]{2,1,0:T(8,128)}, f32[8,64,256]{2,1,0:T(8,128)}, f32[1]{0:T(128)}) custom-call(s32[4]{0:T(128)} %pad_add_fusion.where_ref, f32[256,1,128]{2,1,0:T(1,128)} %copy-done.2, f32[3,256,128]{2,1,0:T(8,128)} %position_ref.1, f32[3,256,128]{2,1,0:T(8,128)} %get-tuple-element.11.velocity_ref, ...), custom_call_target="tpu_custom_call" | custom-call | flops 1000000000 | bytes 8000000 | tf_op jit(solution)/shard_map/sweeps/pallas_call | solution.py:362
  (1 shorter events, 0.0 us)
Async XLA Ops:
  2.4 36.8 %collective-permute-start.1 = (f32[4,32,128]{2,1,0:T(8,128)S(1)}, f32[4,32,128]{2,1,0:T(8,128)S(1)}, u32[]{:S(2)}, u32[]{:S(2)}) collective-permute-start(f32[4,32,128]{2,1,0:T(8,128)S(1)} %get-tuple-element.17), channel_id=1, source_target_pairs={{2,0},{4,2},{6,4},{8,6},{10,8},{12,10},{14,12},{16,14},{18,16},{20... | collective-permute-start | bytes 196616 | tf_op jit(solution)/shard_map/ppermute | solution.py:396
  3.7 35.5 %collective-permute-start = (f32[4,32,128]{2,1,0:T(8,128)S(1)}, f32[4,32,128]{2,1,0:T(8,128)S(1)}, u32[]{:S(2)}, u32[]{:S(2)}) collective-permute-start(f32[4,32,128]{2,1,0:T(8,128)S(1)} %get-tuple-element.18), channel_id=1, source_target_pairs={{0,2},{2,4},{4,6},{6,8},{8,10},{10,12},{12,14},{14,16},{16,18},{18... | collective-permute-start | bytes 196616 | tf_op jit(solution)/shard_map/ppermute | solution.py:395
  8.4 21.8 %copy-start.3 = (s32[256,8]{0,1:T(8,128)S(1)}, s32[256,8]{0,1:T(8,128)}, u32[]{:S(2)}) copy-start(s32[256,8]{0,1:T(8,128)} %param.8) | copy-start | bytes 24580
  8.4 22.7 %copy-start = (f32[3,256,128]{2,1,0:T(8,128)S(1)}, f32[3,256,128]{2,1,0:T(8,128)}, u32[]{:S(2)}) copy-start(f32[3,256,128]{2,1,0:T(8,128)} %position_ref.1) | copy-start | bytes 1179652
  27.1 4.8 %collective-permute-start.2 = (f32[3,8,8,256]{3,2,1,0:T(8,128)}, f32[3,8,8,256]{3,2,1,0:T(8,128)S(1)}, u32[]{:S(2)}, u32[]{:S(2)}) collective-permute-start(f32[3,8,8,256]{3,2,1,0:T(8,128)} %get-tuple-element.13), channel_id=1, source_target_pairs={{0,1},{1,0},{2,3},{3,2},{4,5},{5,4},{6,7},{7,6},{8,9},{9,8},{10,11... | collective-permute-start | bytes 589832 | tf_op jit(solution)/shard_map/ppermute | solution.py:399
  32.6 155.6 %collective-permute-start.4 = (f32[3,8,80,256]{3,2,1,0:T(8,128)}, f32[3,8,80,256]{3,2,1,0:T(8,128)S(1)}, u32[]{:S(2)}, u32[]{:S(2)}) collective-permute-start(f32[3,8,80,256]{3,2,1,0:T(8,128)} %constant_dynamic-update-slice_fusion.own_ref), channel_id=1, source_target_pairs={{2,0},{4,2},{6,4},{8,6},{10,8},{12,10},{14,12},{16,14},{18,16},{20... | collective-permute-start | bytes 5898248 | tf_op jit(solution)/shard_map/ppermute | solution.py:402
  33.9 154.3 %collective-permute-start.3 = (f32[3,8,80,256]{3,2,1,0:T(8,128)}, f32[3,8,80,256]{3,2,1,0:T(8,128)}, u32[]{:S(2)}, u32[]{:S(2)}) collective-permute-start(f32[3,8,80,256]{3,2,1,0:T(8,128)} %constant_dynamic-update-slice_fusion.own_ref), channel_id=1, source_target_pairs={{0,2},{2,4},{4,6},{6,8},{8,10},{10,12},{12,14},{14,16},{16,18},{18... | collective-permute-start | bytes 5898248 | tf_op jit(solution)/shard_map/ppermute | solution.py:401
  39.2 0.6 copy-start.4
  39.8 0.6 copy-start.5
  156.7 31.5 %all-to-all-start = ((f32[256,1,128]{2,1,0:T(1,128)}), f32[256,1,128]{2,1,0:T(1,128)S(1)}, u32[]{:S(2)}, u32[]{:S(2)}) async-start(f32[256,1,128]{2,1,0:T(1,128)} %get-tuple-element.10), calls=%async_computation | async-start | bytes 262144 | tf_op jit(solution)/shard_map/all_to_all | solution.py:415
  188.1 0.7 copy-start.2
  188.1 1.3 copy-start.1

commit v2 on v1

--- a/solution.py
+++ b/solution.py
@@ -31,6 +31,7 @@
 ADHERE_RATIO = ADHERE_STRENGTH / ADHERE_RADIUS**2 / REPEL_FACTOR
 F32 = jnp.float32
 BF16 = jnp.bfloat16
+F8 = jnp.float8_e4m3fn
 VMEM = pltpu.VMEM
 VMEM_LIMIT = 60 * 1024 * 1024
 
@@ -46,9 +47,10 @@
     size_x, size_y, size_z = substrate_ref.shape
     grid_y = size_y * 2
     rows = size_x * size_y
-    group = 8
-    row_id = lax.broadcasted_iota(jnp.int32, (rows, TILE), 0)
-    z_id = lax.broadcasted_iota(jnp.int32, (size_z, TILE), 0)
+    group = 32
+    row_id = lax.broadcasted_iota(jnp.int32, (rows, TILE), 0).astype(jnp.int16)
+    z_id = lax.broadcasted_iota(jnp.int32, (size_z, TILE), 0).astype(jnp.int16)
+    one_hot, no_hot = jnp.ones((), BF16), jnp.zeros((), BF16)
     count[...] = jnp.zeros_like(count)
 
     def step(g, carry):
@@ -64,8 +66,8 @@
             left = []
             right = []
             for i in (pair, pair + 1):
-                left.append(jnp.where(row_id == row[i : i + 1, :], 1.0, 0.0).astype(BF16))
-                right.append(jnp.where(z_id == z[i : i + 1, :], 1.0, 0.0).astype(BF16))
+                left.append(jnp.where(row_id == jnp.broadcast_to(row[i : i + 1, :], row_id.shape).astype(jnp.int16), one_hot, no_hot).astype(F8))
+                right.append(jnp.where(z_id == jnp.broadcast_to(z[i : i + 1, :], z_id.shape).astype(jnp.int16), one_hot, no_hot).astype(F8))
             part = lax.dot_general(
                 jnp.concatenate(left, 1),
                 jnp.concatenate(right, 1),
@@ -257,7 +259,7 @@
                 field[x, half, 8 + rows : 16 + rows, :] = jnp.zeros((8, TILE), F32)
         return carry
 
-    lax.fori_loop(0, 3 * size_x, margins, 0)
+    lax.fori_loop(0, 3 * size_x, margins, 0, unroll=4)
 
     for source, at, present in (
         (before_ref, 0, slab > 0),
@@ -278,7 +280,7 @@
                 factor[at + x, half] = jnp.where(usable, DIFFUSION_NUMBER * inverse, 0.0)
             return carry
 
-        lax.fori_loop(0, size_x, fill, 0)
+        lax.fori_loop(0, size_x, fill, 0, unroll=4)
 
     low_lane = lax.broadcasted_iota(jnp.int32, (rows, TILE), 1) == 0
     high_lane = lax.broadcasted_iota(jnp.int32, (rows, TILE), 1) == TILE - 1
@@ -306,7 +308,8 @@
                     target[x, half, here, :] = value
             return carry
 
-        lax.fori_loop(k + 1, 3 * size_x - k - 1, sweep, 0)
+        planes = 3 * size_x - 2 * k - 2
+        lax.fori_loop(k + 1, 3 * size_x - k - 1, sweep, 0, unroll=planes // 2)
 
 
 WHOLE = pl.BlockSpec(memory_space=pltpu.VMEM)

time: 209 us -> 191 us (0.914)
  Pallas kernels: 154 us -> 136 us
    pallas_call x1, Pallas kernels: 18.7 us -> 8.53 us  [counts(): pl.pallas_call(count_kernel, out_shape=(jax.ShapeDtypeStruct((3, size_x,...]
    pallas_call x1, Pallas kernels: 19 us -> 11.6 us  [sweeps(): pl.pallas_call(sweep_kernel, out_shape=(jax.ShapeDtypeStruct(position.sha...]
  transfers between devices with their start and end apart: 6 -> 6, of which waited for: 1 -> 1; matrix products, arithmetic and copies ran while one was open for 1% -> 2% of each run, Pallas kernels for 65% -> 65%
where the time goes in v2:
time: 191 us
  Pallas kernels  136 us (71%)
  starting transfers between devices  34.3 us (18%)
  waiting for transfers between devices  12.2 us (6%)
  local copies, waits for them, and re-layouts  4.07 us (2%)
  other arithmetic  3.2 us (2%)
    pallas_call x1, Pallas kernels, forces(): pl.pallas_call(force_kernel, out_shape=(jax.ShapeDtypeStruct((3, tiles_de...  116 us
    all_to_all x1, starting transfers between devices, body(): stats = lax.all_to_all(stats, SLAB_SUB, 0, 0, tiled=True)  18.7 us
    all_to_all x1, waiting for transfers between devices, body(): stats = lax.all_to_all(stats, SLAB_SUB, 0, 0, tiled=True)  12.2 us
    pallas_call x1, Pallas kernels, sweeps(): pl.pallas_call(sweep_kernel, out_shape=(jax.ShapeDtypeStruct(position.sha...  11.6 us
    pallas_call x1, Pallas kernels, counts(): pl.pallas_call(count_kernel, out_shape=(jax.ShapeDtypeStruct((3, size_x,...  8.53 us
    ppermute x1, starting transfers between devices, body(): field_before = lax.ppermute(own, SLAB, up)  5.3 us
    ppermute x1, starting transfers between devices, body(): ghost_before = lax.ppermute(codes[:, tiles_dev - GHOST:], SLAB, up)  4.65 us
  transfers between devices with their start and end apart: 6, of which 1 were waited for; matrix products, arithmetic and copies ran while one was open for 2% of the time, Pallas kernels for 65%

profile of v2, /device:TPU:1, one launch (start us, length us, event | category | flops | bytes accessed | tf_op | source)
XLA Modules:
  0.0 190.8 jit_solution(1078004274414342483)
XLA Ops:
  0.6 0.9 convert_bitcast_fusion
  1.5 0.8 fusion.1
  2.4 1.3 collective-permute-start.1
  3.7 4.7 %collective-permute-start = (f32[4,32,128]{2,1,0:T(8,128)S(1)}, f32[4,32,128]{2,1,0:T(8,128)S(1)}, u32[]{:S(2)}, u32[]{:S(2)}) collective-permute-start(f32[4,32,128]{2,1,0:T(8,128)S(1)} %get-tuple-element.18), channel_id=1, source_target_pairs={{0,2},{2,4},{4,6},{6,8},{8,10},{10,12},{12,14},{14,16},{16,18},{18... | collective-permute-start | bytes 196616 | tf_op jit(solution)/shard_map/ppermute | solution.py:398
  8.4 0.0 copy-start.3
  8.4 0.0 copy-start
  8.4 8.5 %counts.1 = (f32[3,8,80,256]{3,2,1,0:T(8,128)}, f32[3,8,8,256]{3,2,1,0:T(8,128)}) custom-call(s32[1]{0:T(128)} %bitcast.1.sub_ref, s32[256,128]{1,0:T(8,128)} %voxel_ref.1, s32[256,128]{1,0:T(8,128)} %state_ref.1, f32[8,64,256]{2,1,0:T(8,128)} %substrate_ref.1, f32[8,64,256]{2,1,0:T(8,128)} %secretion_ref.1), custom_call_target="tpu_custom_call" | custom-call | flops 8999999488 | bytes 4000000 | tf_op jit(solution)/shard_map/counts/pallas_call | solution.py:321
  16.9 3.1 %collective-permute-start.2 = (f32[3,8,8,256]{3,2,1,0:T(8,128)}, f32[3,8,8,256]{3,2,1,0:T(8,128)S(1)}, u32[]{:S(2)}, u32[]{:S(2)}) collective-permute-start(f32[3,8,8,256]{3,2,1,0:T(8,128)} %get-tuple-element.13), channel_id=1, source_target_pairs={{0,1},{1,0},{2,3},{3,2},{4,5},{5,4},{6,7},{7,6},{8,9},{9,8},{10,11... | collective-permute-start | bytes 589832 | tf_op jit(solution)/shard_map/ppermute | solution.py:402
  20.0 0.0 copy-done.3
  20.0 0.1 copy.9
  20.2 0.7 reshape.13.ids_ref
  20.9 0.0 copy-done
  20.9 0.8 pad_maximum_fusion.own_ref
  21.7 0.0 collective-permute-done.2
  21.7 0.7 constant_dynamic-update-slice_fusion.own_ref
  22.4 1.3 collective-permute-start.4
  23.7 5.3 %collective-permute-start.3 = (f32[3,8,80,256]{3,2,1,0:T(8,128)}, f32[3,8,80,256]{3,2,1,0:T(8,128)}, u32[]{:S(2)}, u32[]{:S(2)}) collective-permute-start(f32[3,8,80,256]{3,2,1,0:T(8,128)} %constant_dynamic-update-slice_fusion.own_ref), channel_id=1, source_target_pairs={{0,2},{2,4},{4,6},{6,8},{8,10},{10,12},{12,14},{14,16},{16,18},{18... | collective-permute-start | bytes 5898248 | tf_op jit(solution)/shard_map/ppermute | solution.py:404
  29.0 0.0 collective-permute-done.1.after_ref
  29.0 0.0 copy-start.4
  29.0 0.0 collective-permute-done.before_ref
  29.0 0.6 copy-done.4
  29.6 0.0 copy-start.5
  29.6 0.6 copy-done.5
  30.2 116.3 %forces.1 = (f32[3,256,128]{2,1,0:T(8,128)}, f32[256,1,128]{2,1,0:T(1,128)}) custom-call(s32[2048]{0:T(1024)} %reshape.13.ids_ref, f32[4,256,128]{2,1,0:T(8,128)} %pad_maximum_fusion.own_ref, f32[4,32,128]{2,1,0:T(8,128)} %copy-done.5, f32[4,32,128]{2,1,0:T(8,128)} %copy-done.4), custom_call_target="tpu_custom_call" | custom-call | flops 99999997952 | bytes 1000000 | tf_op jit(solution)/shard_map/forces/pallas_call | solution.py:339
  146.5 18.7 %all-to-all-start = ((f32[256,1,128]{2,1,0:T(1,128)}), f32[256,1,128]{2,1,0:T(1,128)S(1)}, u32[]{:S(2)}, u32[]{:S(2)}) async-start(f32[256,1,128]{2,1,0:T(1,128)} %get-tuple-element.10), calls=%async_computation | async-start | bytes 262144 | tf_op jit(solution)/shard_map/all_to_all | solution.py:418
  165.2 0.6 pad_add_fusion.where_ref
  165.8 12.2 %all-to-all-done.stats_ref = f32[256,1,128]{2,1,0:T(1,128)S(1)} async-done(((f32[256,1,128]{2,1,0:T(1,128)}), f32[256,1,128]{2,1,0:T(1,128)S(1)}, u32[]{:S(2)}, u32[]{:S(2)}) %all-to-all-start) | async-done | bytes 131104 | tf_op jit(solution)/shard_map/all_to_all | solution.py:418
  177.9 0.0 copy-start.2
  178.0 0.0 collective-permute-done.4.after_ref
  178.0 0.0 copy-start.1
  178.0 0.0 collective-permute-done.3.before_ref
  178.0 0.6 copy-done.2
  178.6 0.7 copy-done.1
  179.3 11.6 %sweeps.1 = (f32[3,256,128]{2,1,0:T(8,128)}, f32[8,64,256]{2,1,0:T(8,128)}, f32[1]{0:T(128)}) custom-call(s32[4]{0:T(128)} %pad_add_fusion.where_ref, f32[256,1,128]{2,1,0:T(1,128)} %copy-done.2, f32[3,256,128]{2,1,0:T(8,128)} %position_ref.1, f32[3,256,128]{2,1,0:T(8,128)} %get-tuple-element.11.velocity_ref, ...), custom_call_target="tpu_custom_call" | custom-call | flops 1000000000 | bytes 8000000 | tf_op jit(solution)/shard_map/sweeps/pallas_call | solution.py:365
  (1 shorter events, 0.0 us)
Async XLA Ops:
  2.4 26.6 %collective-permute-start.1 = (f32[4,32,128]{2,1,0:T(8,128)S(1)}, f32[4,32,128]{2,1,0:T(8,128)S(1)}, u32[]{:S(2)}, u32[]{:S(2)}) collective-permute-start(f32[4,32,128]{2,1,0:T(8,128)S(1)} %get-tuple-element.17), channel_id=1, source_target_pairs={{2,0},{4,2},{6,4},{8,6},{10,8},{12,10},{14,12},{16,14},{18,16},{20... | collective-permute-start | bytes 196616 | tf_op jit(solution)/shard_map/ppermute | solution.py:399
  3.7 25.3 %collective-permute-start = (f32[4,32,128]{2,1,0:T(8,128)S(1)}, f32[4,32,128]{2,1,0:T(8,128)S(1)}, u32[]{:S(2)}, u32[]{:S(2)}) collective-permute-start(f32[4,32,128]{2,1,0:T(8,128)S(1)} %get-tuple-element.18), channel_id=1, source_target_pairs={{0,2},{2,4},{4,6},{6,8},{8,10},{10,12},{12,14},{14,16},{16,18},{18... | collective-permute-start | bytes 196616 | tf_op jit(solution)/shard_map/ppermute | solution.py:398
  8.4 11.7 %copy-start.3 = (s32[256,8]{0,1:T(8,128)S(1)}, s32[256,8]{0,1:T(8,128)}, u32[]{:S(2)}) copy-start(s32[256,8]{0,1:T(8,128)} %param.8) | copy-start | bytes 24580
  8.4 12.5 %copy-start = (f32[3,256,128]{2,1,0:T(8,128)S(1)}, f32[3,256,128]{2,1,0:T(8,128)}, u32[]{:S(2)}) copy-start(f32[3,256,128]{2,1,0:T(8,128)} %position_ref.1) | copy-start | bytes 1179652
  16.9 4.8 %collective-permute-start.2 = (f32[3,8,8,256]{3,2,1,0:T(8,128)}, f32[3,8,8,256]{3,2,1,0:T(8,128)S(1)}, u32[]{:S(2)}, u32[]{:S(2)}) collective-permute-start(f32[3,8,8,256]{3,2,1,0:T(8,128)} %get-tuple-element.13), channel_id=1, source_target_pairs={{0,1},{1,0},{2,3},{3,2},{4,5},{5,4},{6,7},{7,6},{8,9},{9,8},{10,11... | collective-permute-start | bytes 589832 | tf_op jit(solution)/shard_map/ppermute | solution.py:402
  22.4 155.6 %collective-permute-start.4 = (f32[3,8,80,256]{3,2,1,0:T(8,128)}, f32[3,8,80,256]{3,2,1,0:T(8,128)S(1)}, u32[]{:S(2)}, u32[]{:S(2)}) collective-permute-start(f32[3,8,80,256]{3,2,1,0:T(8,128)} %constant_dynamic-update-slice_fusion.own_ref), channel_id=1, source_target_pairs={{2,0},{4,2},{6,4},{8,6},{10,8},{12,10},{14,12},{16,14},{18,16},{20... | collective-permute-start | bytes 5898248 | tf_op jit(solution)/shard_map/ppermute | solution.py:405
  23.7 154.3 %collective-permute-start.3 = (f32[3,8,80,256]{3,2,1,0:T(8,128)}, f32[3,8,80,256]{3,2,1,0:T(8,128)}, u32[]{:S(2)}, u32[]{:S(2)}) collective-permute-start(f32[3,8,80,256]{3,2,1,0:T(8,128)} %constant_dynamic-update-slice_fusion.own_ref), channel_id=1, source_target_pairs={{0,2},{2,4},{4,6},{6,8},{8,10},{10,12},{12,14},{14,16},{16,18},{18... | collective-permute-start | bytes 5898248 | tf_op jit(solution)/shard_map/ppermute | solution.py:404
  29.0 0.6 copy-start.4
  29.6 0.6 copy-start.5
  146.5 31.5 %all-to-all-start = ((f32[256,1,128]{2,1,0:T(1,128)}), f32[256,1,128]{2,1,0:T(1,128)S(1)}, u32[]{:S(2)}, u32[]{:S(2)}) async-start(f32[256,1,128]{2,1,0:T(1,128)} %get-tuple-element.10), calls=%async_computation | async-start | bytes 262144 | tf_op jit(solution)/shard_map/all_to_all | solution.py:418
  177.9 0.7 copy-start.2
  178.0 1.3 copy-start.1

commit v3 on v2

--- a/solution.py
+++ b/solution.py
@@ -1,3 +1,5 @@
+import functools
+
 import jax
 import jax.numpy as jnp
 from jax import lax
@@ -26,6 +28,7 @@
 UPTAKE_SCALE = 0.25
 
 FEATURES = 32
+ROW_CHOICES = (48, 64, 80, 96, 112, 128)
 FAR = float(2**20)
 REPEL_FACTOR = REPEL_STRENGTH / REPEL_RADIUS**2
 ADHERE_RATIO = ADHERE_STRENGTH / ADHERE_RADIUS**2 / REPEL_FACTOR
@@ -87,7 +90,7 @@
 
 
 def force_kernel(
-    ids_ref, own_ref, before_ref, after_ref, velocity_ref, stats_ref,
+    ids_ref, own_ref, state_ref, before_ref, after_ref, velocity_ref, stats_ref,
     features, adhere, weights, left_rows, right_rows, even, odd,
 ):
     tiles = own_ref.shape[1]
@@ -99,8 +102,19 @@
     zero = jnp.zeros((8, TILE), F32)
     one = jnp.ones((8, TILE), F32)
 
-    def put_left(source, at, target):
-        state = source[3, pl.ds(at, 8), :]
+    slot = lax.broadcasted_iota(jnp.int32, (8, TILE), 1).astype(F32)
+    earlier = jnp.where(
+        lax.broadcasted_iota(jnp.int32, (TILE, TILE), 0) < lax.broadcasted_iota(jnp.int32, (TILE, TILE), 1),
+        1.0,
+        0.0,
+    ).astype(BF16)
+    place = lax.broadcasted_iota(jnp.int32, (TILE, TILE), 0)
+
+    def put_left(source, state, at, target, fullest):
+        occupied = jnp.where(state > 0.5, 1.0, 0.0)
+        ahead = jnp.dot(occupied.astype(BF16), earlier, preferred_element_type=F32)
+        total = jnp.sum(occupied, 1, keepdims=True)
+        order = jnp.where(state > 0.5, ahead, total + slot - ahead).astype(jnp.int32)
         live = jnp.where(state == 1.0, 1.0, 0.0)
         vacant = jnp.where(state > 0.5, 0.0, FAR)
         norm = zero
@@ -116,10 +130,14 @@
         for k, row in enumerate(rows):
             left_rows[k * 8 : k * 8 + 8, :] = row
         for i in range(8):
-            block = left_rows[pl.ds(i, FEATURES, stride=8), :]
-            turned = block.T.astype(BF16)
+            block = left_rows[pl.ds(i, FEATURES, stride=8), :].astype(BF16)
+            chosen = jnp.where(place == order[i : i + 1, :], 1.0, 0.0).astype(BF16)
+            turned = lax.dot_general(
+                chosen, block, (((1,), (1,)), ((), ())), preferred_element_type=F32
+            ).astype(BF16)
             features[target + i] = turned
             adhere[target + i] = jnp.dot(turned, ratio_rows, preferred_element_type=F32)
+        return jnp.maximum(fullest, ahead + occupied)
 
     def put_right(at):
         norm = jnp.full((8, TILE), SOFTENING, F32)
@@ -154,72 +172,79 @@
 
     def ghosts(g, carry):
         at = pl.multiple_of(g * 8, 8)
-        put_left(before_ref, at, at)
-        put_left(after_ref, at, at + GHOST + tiles)
-        return carry
+        carry = put_left(before_ref, before_ref[3, pl.ds(at, 8), :], at, at, carry)
+        return put_left(after_ref, after_ref[3, pl.ds(at, 8), :], at, at + GHOST + tiles, carry)
 
     def owned(g, carry):
         at = pl.multiple_of(g * 8, 8)
-        put_left(own_ref, at, at + GHOST)
+        carry = put_left(own_ref, state_ref[pl.ds(at, 8), :].astype(F32), at, at + GHOST, carry)
         put_right(at)
         return carry
 
-    lax.fori_loop(0, GHOST // 8, ghosts, 0)
-    lax.fori_loop(0, tiles // 8, owned, 0)
-
-    def products(tile, j, target):
-        other = ids_ref[tile * NB + j]
-        target[j * TILE : (j + 1) * TILE, :] = jnp.dot(
-            features[other], weights[tile], preferred_element_type=F32
-        )
-
-    def pairs(tile, j, source, reach, total):
-        other = ids_ref[tile * NB + j]
-        chunk = 32
-        for c in range(0, TILE, chunk):
-            rows = slice(j * TILE + c, j * TILE + c + chunk)
-            square = source[rows, 0:TILE]
-            inverse = lax.rsqrt(square)
-            distance = square * inverse
-            near = jnp.maximum(REPEL_RADIUS - distance, 0.0)
-            far = jnp.maximum(reach - distance, 0.0)
-            weight = (near * near - adhere[other, c : c + chunk, :] * (far * far)) * inverse
+    fullest = lax.fori_loop(0, GHOST // 8, ghosts, zero, unroll=2)
+    fullest = lax.fori_loop(0, tiles // 8, owned, fullest, unroll=4)
+    needed = jnp.max(fullest)
+
+    def run(rows):
+        chunk = 16
+
+        def products(tile, j, target):
+            other = ids_ref[tile * NB + j]
+            target[j * rows : (j + 1) * rows, :] = jnp.dot(
+                features[other, 0:rows, :], weights[tile], preferred_element_type=F32
+            )
+
+        def pairs(tile, j, source, reach, total):
+            other = ids_ref[tile * NB + j]
+            for c in range(0, rows, chunk):
+                at = slice(j * rows + c, j * rows + c + chunk)
+                square = source[at, 0:TILE]
+                inverse = lax.rsqrt(square)
+                distance = square * inverse
+                near = jnp.maximum(REPEL_RADIUS - distance, 0.0)
+                far = jnp.maximum(reach - distance, 0.0)
+                weight = (near * near - adhere[other, c : c + chunk, :] * (far * far)) * inverse
+                for axis in range(3):
+                    term = weight * source[at, (axis + 1) * TILE : (axis + 2) * TILE]
+                    total[axis] = total[axis] + jnp.sum(term.reshape(chunk // 8, 8, TILE), 0)
+            return total
+
+        def one_tile(tile, following, source, target):
+            live = state_ref[pl.ds(tile, 1), :] == 1
+            reach = jnp.broadcast_to(jnp.where(live, ADHERE_RADIUS, -1.0), (chunk, TILE))
+            total = [zero, zero, zero]
+            for j in range(NB):
+                products(following, j, target)
+                total = pairs(tile, j, source, reach, total)
             for axis in range(3):
-                term = weight * source[rows, (axis + 1) * TILE : (axis + 2) * TILE]
-                total[axis] = total[axis] + jnp.sum(term.reshape(chunk // 8, 8, TILE), 0)
-        return total
-
-    def one_tile(tile, following, source, target):
-        live = own_ref[3, pl.ds(tile, 1), :] == 1.0
-        reach = jnp.broadcast_to(jnp.where(live, ADHERE_RADIUS, -1.0), (32, TILE))
-        total = [zero, zero, zero]
+                velocity_ref[axis, pl.ds(tile, 1), :] = jnp.sum(total[axis], 0, keepdims=True)
+
         for j in range(NB):
-            products(following, j, target)
-            total = pairs(tile, j, source, reach, total)
-        for axis in range(3):
-            velocity_ref[axis, pl.ds(tile, 1), :] = jnp.sum(total[axis], 0, keepdims=True)
-
-    for j in range(NB):
-        products(0, j, even)
-
-    def two_tiles(i, carry):
-        tile = i * 2
-        one_tile(tile, tile + 1, even, odd)
-        one_tile(tile + 1, jnp.minimum(tile + 2, tiles - 1), odd, even)
-        return carry
-
-    lax.fori_loop(0, tiles // 2, two_tiles, 0)
-
-    state = own_ref[3]
-    scale = jnp.where(state > 0.5, REPEL_FACTOR, 0.0)
+            products(0, j, even)
+
+        def two_tiles(i, carry):
+            tile = i * 2
+            one_tile(tile, tile + 1, even, odd)
+            one_tile(tile + 1, jnp.minimum(tile + 2, tiles - 1), odd, even)
+            return carry
+
+        lax.fori_loop(0, tiles // 2, two_tiles, 0)
+
+    below = -1.0
+    for rows in ROW_CHOICES:
+        pl.when((needed > below) & (needed <= rows))(functools.partial(run, rows))
+        below = float(rows)
+
+    state = state_ref[...]
+    scale = jnp.where(state > 0, REPEL_FACTOR, 0.0)
     speed = jnp.zeros((tiles, TILE), F32)
     for axis in range(3):
         value = velocity_ref[axis] * scale
         velocity_ref[axis] = value
         speed = speed + value * value
     fastest = jnp.max(jnp.sqrt(speed))
-    live = jnp.sum(jnp.where(state == 1.0, 1.0, 0.0))
-    necrotic = jnp.sum(jnp.where(state == 2.0, 1.0, 0.0))
+    live = jnp.sum(jnp.where(state == 1, 1.0, 0.0))
+    necrotic = jnp.sum(jnp.where(state == 2, 1.0, 0.0))
     lane = lax.broadcasted_iota(jnp.int32, stats_ref.shape, 2)
     stats_ref[...] = jnp.where(lane == 0, fastest, jnp.where(lane == 1, live, necrotic))
 
@@ -333,8 +358,8 @@
     )(sub_index, voxel, state, substrate, secretion)
 
 
-def forces(local_ids, codes, ghost_before, ghost_after, devices):
-    tiles_dev = codes.shape[1]
+def forces(local_ids, position, state, ghost_before, ghost_after, devices):
+    tiles_dev = position.shape[1]
     all_tiles = tiles_dev + 2 * GHOST
     return pl.pallas_call(
         force_kernel,
@@ -342,7 +367,7 @@
             jax.ShapeDtypeStruct((3, tiles_dev, TILE), F32),
             jax.ShapeDtypeStruct((devices, 1, TILE), F32),
         ),
-        in_specs=[SCALAR] + [WHOLE] * 3,
+        in_specs=[SCALAR] + [WHOLE] * 4,
         out_specs=(WHOLE, WHOLE),
         scratch_shapes=[
             VMEM((all_tiles, TILE, FEATURES), BF16),
@@ -356,7 +381,7 @@
         compiler_params=pltpu.CompilerParams(vmem_limit_bytes=VMEM_LIMIT),
         cost_estimate=pl.CostEstimate(flops=10**11, bytes_accessed=10**6, transcendentals=0),
         name="forces",
-    )(local_ids, codes, ghost_before, ghost_after)
+    )(local_ids, position, state, ghost_before, ghost_after)
 
 
 def sweeps(location, stats, position, velocity, before, own, after):
@@ -394,9 +419,11 @@
     up = [(i, i + 1) for i in range(slab_count - 1)]
     down = [(i + 1, i) for i in range(slab_count - 1)]
 
-    codes = jnp.concatenate([position, state.astype(F32)[None]], 0)
-    ghost_before = lax.ppermute(codes[:, tiles_dev - GHOST :], SLAB, up)
-    ghost_after = lax.ppermute(codes[:, :GHOST], SLAB, down)
+    def codes(tiles):
+        return jnp.concatenate([position[:, tiles], state[tiles].astype(F32)[None]], 0)
+
+    ghost_before = lax.ppermute(codes(slice(tiles_dev - GHOST, tiles_dev)), SLAB, up)
+    ghost_after = lax.ppermute(codes(slice(0, GHOST)), SLAB, down)
 
     own, edge = counts(sub_index.reshape(1), voxel, state, substrate, secretion)
     other = lax.ppermute(edge, "sub", [(0, 1), (1, 0)])
@@ -414,7 +441,9 @@
             GHOST + neighbours - first_tile,
         ),
     ).reshape(-1)
-    velocity, stats = forces(local_ids, codes, ghost_before, ghost_after, slab_count * sub_count)
+    velocity, stats = forces(
+        local_ids, position, state, ghost_before, ghost_after, slab_count * sub_count
+    )
     stats = lax.all_to_all(stats, SLAB_SUB, 0, 0, tiled=True)
     location = jnp.stack([slab_index, jnp.int32(slab_count), jnp.int32(sub_count), sub_index])
     new_position, new_substrate, fraction = sweeps(

time: 191 us -> 185 us (0.969)
  Pallas kernels: 136 us -> 95.8 us
  starting transfers between devices: 34.3 us -> 68.8 us
    pallas_call x1, Pallas kernels: 116 us -> 75.8 us  [forces(): pl.pallas_call(force_kernel, out_shape=(jax.ShapeDtypeStruct((3, tiles_de...]
    all_to_all x1, starting transfers between devices: 18.7 us -> 55.1 us  [body(): stats = lax.all_to_all(stats, SLAB_SUB, 0, 0, tiled=True)]
    ppermute x1, starting transfers between devices: 3.1 us -> 0.96 us  [body(): other = lax.ppermute(edge, 'sub', [(0, 1), (1, 0)])]
  transfers between devices with their start and end apart: 6 -> 6, of which waited for: 1 -> 2; matrix products, arithmetic and copies ran while one was open for 2% -> 1% of each run, Pallas kernels for 65% -> 46%
where the time goes in v3:
time: 185 us; the launch traced here: 184 us
  Pallas kernels  95.8 us (52%)
  starting transfers between devices  68.8 us (37%)
  waiting for transfers between devices  12.6 us (7%)
  local copies, waits for them, and re-layouts  4.9 us (3%)
    pallas_call x1, Pallas kernels, forces(): pl.pallas_call(force_kernel, out_shape=(jax.ShapeDtypeStruct((3, tiles_de...  75.8 us
    all_to_all x1, starting transfers between devices, body(): stats = lax.all_to_all(stats, SLAB_SUB, 0, 0, tiled=True)  55.1 us
    all_to_all x1, waiting for transfers between devices, body(): stats = lax.all_to_all(stats, SLAB_SUB, 0, 0, tiled=True)  12.2 us
    pallas_call x1, Pallas kernels, sweeps(): pl.pallas_call(sweep_kernel, out_shape=(jax.ShapeDtypeStruct(position.sha...  11.6 us
    pallas_call x1, Pallas kernels, counts(): pl.pallas_call(count_kernel, out_shape=(jax.ShapeDtypeStruct((3, size_x,...  8.49 us
    ppermute x1, starting transfers between devices, body(): field_before = lax.ppermute(own, SLAB, up)  6.21 us
    ppermute x1, starting transfers between devices, body(): lax.ppermute(codes(slice(tiles_dev - GHOST, tiles_dev)), SLAB, up)  4.02 us
  transfers between devices with their start and end apart: 6, of which 2 were waited for; matrix products, arithmetic and copies ran while one was open for 1% of the time, Pallas kernels for 46%

profile of v3, /device:TPU:1, one launch (start us, length us, event | category | flops | bytes accessed | tf_op | source)
XLA Modules:
  0.0 184.4 jit_solution(9998225184495456298)
XLA Ops:
  0.6 0.7 convert_bitcast_fusion
  1.4 0.8 fusion
  2.2 4.0 %collective-permute-start = (f32[4,32,128]{2,1,0:T(8,128)S(1)}, f32[4,32,128]{2,1,0:T(8,128)S(1)}, u32[]{:S(2)}, u32[]{:S(2)}) collective-permute-start(f32[4,32,128]{2,1,0:T(8,128)S(1)} %pad_maximum_fusion), channel_id=1, source_target_pairs={{0,2},{2,4},{4,6},{6,8},{8,10},{10,12},{12,14},{14,16},{16,18},{18... | collective-permute-start | bytes 196616 | tf_op jit(solution)/shard_map/ppermute | solution.py:425
  6.3 1.3 collective-permute-start.1
  7.6 0.0 copy-start.2
  7.6 8.5 %counts.1 = (f32[3,8,80,256]{3,2,1,0:T(8,128)}, f32[3,8,8,256]{3,2,1,0:T(8,128)}) custom-call(s32[1]{0:T(128)} %bitcast.1.sub_ref, s32[256,128]{1,0:T(8,128)} %voxel_ref.1, s32[256,128]{1,0:T(8,128)} %state_ref.3, f32[8,64,256]{2,1,0:T(8,128)} %substrate_ref.1, f32[8,64,256]{2,1,0:T(8,128)} %secretion_ref.1), custom_call_target="tpu_custom_call" | custom-call | flops 8999999488 | bytes 4000000 | tf_op jit(solution)/shard_map/counts/pallas_call | solution.py:346
  16.1 1.0 collective-permute-start.2
  17.0 0.0 copy-done.2
  17.0 0.1 copy.9
  17.2 0.7 reshape.13.ids_ref
  17.9 0.4 collective-permute-done.2
  18.3 0.7 constant_dynamic-update-slice_fusion.own_ref
  19.0 1.3 collective-permute-start.4
  20.3 6.2 %collective-permute-start.3 = (f32[3,8,80,256]{3,2,1,0:T(8,128)}, f32[3,8,80,256]{3,2,1,0:T(8,128)}, u32[]{:S(2)}, u32[]{:S(2)}) collective-permute-start(f32[3,8,80,256]{3,2,1,0:T(8,128)} %constant_dynamic-update-slice_fusion.own_ref), channel_id=1, source_target_pairs={{0,2},{2,4},{4,6},{6,8},{8,10},{10,12},{12,14},{14,16},{16,18},{18... | collective-permute-start | bytes 5898248 | tf_op jit(solution)/shard_map/ppermute | solution.py:431
  26.5 0.0 collective-permute-done.before_ref
  26.5 0.0 copy-start.3
  26.5 0.0 collective-permute-done.1.after_ref
  26.5 0.6 copy-done.3
  27.1 0.0 copy-start.4
  27.1 0.6 copy-done.4
  27.7 75.8 %forces.1 = (f32[3,256,128]{2,1,0:T(8,128)}, f32[256,1,128]{2,1,0:T(1,128)}) custom-call(s32[2048]{0:T(1024)} %reshape.13.ids_ref, f32[3,256,128]{2,1,0:T(8,128)} %position_ref.1, s32[256,128]{1,0:T(8,128)} %state_ref.3, f32[4,32,128]{2,1,0:T(8,128)} %copy-done.3, f32[4,32,128]{2,1,0:T(8,128)} %copy-done.4), custom_call_target="tpu_custom_call" | custom-call | flops 99999997952 | bytes 1000000 | tf_op jit(solution)/shard_map/forces/pallas_call | solution.py:364
  103.5 55.1 %all-to-all-start = ((f32[256,1,128]{2,1,0:T(1,128)}), f32[256,1,128]{2,1,0:T(1,128)S(1)}, u32[]{:S(2)}, u32[]{:S(2)}) async-start(f32[256,1,128]{2,1,0:T(1,128)} %get-tuple-element.10), calls=%async_computation | async-start | bytes 262144 | tf_op jit(solution)/shard_map/all_to_all | solution.py:447
  158.6 0.6 pad_add_fusion.where_ref
  159.2 12.2 %all-to-all-done.stats_ref = f32[256,1,128]{2,1,0:T(1,128)S(1)} async-done(((f32[256,1,128]{2,1,0:T(1,128)}), f32[256,1,128]{2,1,0:T(1,128)S(1)}, u32[]{:S(2)}, u32[]{:S(2)}) %all-to-all-start) | async-done | bytes 131104 | tf_op jit(solution)/shard_map/all_to_all | solution.py:447
  171.4 0.0 copy-start.1
  171.4 0.0 collective-permute-done.4.after_ref
  171.4 0.0 copy-start
  171.4 0.0 collective-permute-done.3.before_ref
  171.4 0.6 copy-done.1
  172.0 0.7 copy-done
  172.7 11.6 %sweeps.1 = (f32[3,256,128]{2,1,0:T(8,128)}, f32[8,64,256]{2,1,0:T(8,128)}, f32[1]{0:T(128)}) custom-call(s32[4]{0:T(128)} %pad_add_fusion.where_ref, f32[256,1,128]{2,1,0:T(1,128)} %copy-done.1, f32[3,256,128]{2,1,0:T(8,128)} %position_ref.1, f32[3,256,128]{2,1,0:T(8,128)} %get-tuple-element.11.velocity_ref, ...), custom_call_target="tpu_custom_call" | custom-call | flops 1000000000 | bytes 8000000 | tf_op jit(solution)/shard_map/sweeps/pallas_call | solution.py:390
  (3 shorter events, 0.0 us)
Async XLA Ops:
  2.2 24.3 %collective-permute-start = (f32[4,32,128]{2,1,0:T(8,128)S(1)}, f32[4,32,128]{2,1,0:T(8,128)S(1)}, u32[]{:S(2)}, u32[]{:S(2)}) collective-permute-start(f32[4,32,128]{2,1,0:T(8,128)S(1)} %pad_maximum_fusion), channel_id=1, source_target_pairs={{0,2},{2,4},{4,6},{6,8},{8,10},{10,12},{12,14},{14,16},{16,18},{18... | collective-permute-start | bytes 196616 | tf_op jit(solution)/shard_map/ppermute | solution.py:425
  6.3 20.2 %collective-permute-start.1 = (f32[4,32,128]{2,1,0:T(8,128)S(1)}, f32[4,32,128]{2,1,0:T(8,128)S(1)}, u32[]{:S(2)}, u32[]{:S(2)}) collective-permute-start(f32[4,32,128]{2,1,0:T(8,128)S(1)} %pad_maximum_fusion.1), channel_id=1, source_target_pairs={{2,0},{4,2},{6,4},{8,6},{10,8},{12,10},{14,12},{16,14},{18,16},{20... | collective-permute-start | bytes 196616 | tf_op jit(solution)/shard_map/ppermute | solution.py:426
  7.6 9.5 %copy-start.2 = (s32[256,8]{0,1:T(8,128)S(1)}, s32[256,8]{0,1:T(8,128)}, u32[]{:S(2)}) copy-start(s32[256,8]{0,1:T(8,128)} %param.8) | copy-start | bytes 24580
  16.1 2.2 %collective-permute-start.2 = (f32[3,8,8,256]{3,2,1,0:T(8,128)}, f32[3,8,8,256]{3,2,1,0:T(8,128)S(1)}, u32[]{:S(2)}, u32[]{:S(2)}) collective-permute-start(f32[3,8,8,256]{3,2,1,0:T(8,128)} %get-tuple-element.13), channel_id=1, source_target_pairs={{0,1},{1,0},{2,3},{3,2},{4,5},{5,4},{6,7},{7,6},{8,9},{9,8},{10,11... | collective-permute-start | bytes 589832 | tf_op jit(solution)/shard_map/ppermute | solution.py:429
  19.0 152.4 %collective-permute-start.4 = (f32[3,8,80,256]{3,2,1,0:T(8,128)}, f32[3,8,80,256]{3,2,1,0:T(8,128)S(1)}, u32[]{:S(2)}, u32[]{:S(2)}) collective-permute-start(f32[3,8,80,256]{3,2,1,0:T(8,128)} %constant_dynamic-update-slice_fusion.own_ref), channel_id=1, source_target_pairs={{2,0},{4,2},{6,4},{8,6},{10,8},{12,10},{14,12},{16,14},{18,16},{20... | collective-permute-start | bytes 5898248 | tf_op jit(solution)/shard_map/ppermute | solution.py:432
  20.3 151.1 %collective-permute-start.3 = (f32[3,8,80,256]{3,2,1,0:T(8,128)}, f32[3,8,80,256]{3,2,1,0:T(8,128)}, u32[]{:S(2)}, u32[]{:S(2)}) collective-permute-start(f32[3,8,80,256]{3,2,1,0:T(8,128)} %constant_dynamic-update-slice_fusion.own_ref), channel_id=1, source_target_pairs={{0,2},{2,4},{4,6},{6,8},{8,10},{10,12},{12,14},{14,16},{16,18},{18... | collective-permute-start | bytes 5898248 | tf_op jit(solution)/shard_map/ppermute | solution.py:431
  26.5 0.6 copy-start.3
  27.1 0.6 copy-start.4
  103.5 67.8 %all-to-all-start = ((f32[256,1,128]{2,1,0:T(1,128)}), f32[256,1,128]{2,1,0:T(1,128)S(1)}, u32[]{:S(2)}, u32[]{:S(2)}) async-start(f32[256,1,128]{2,1,0:T(1,128)} %get-tuple-element.10), calls=%async_computation | async-start | bytes 262144 | tf_op jit(solution)/shard_map/all_to_all | solution.py:447
  171.4 0.7 copy-start.1
  171.4 1.3 copy-start
